TPU v7x, 128 devices: a whole 4x4x4 slice. The times are simulated.
128 devices in a mesh: gx: 4 (over z), gy: 4 (over y), gz: 8 (over x, core).
Axes of the slice: x: 4, y: 4, z: 4, core: 2. Of those that a mesh axis runs over, the one named last changes fastest.
Arguments:
- positions: float32 [3, 64, 64, 2048], P(None, 'gx', 'gy', 'gz'), may hold values from -6 to 6
- pair_node: int32 [4, 4, 8, 32, 256], P('gx', 'gy', 'gz'), may hold values from 0 to 255
- pair_line: int32 [4, 4, 8, 32], P('gx', 'gy', 'gz'), may hold values from 0 to 255
- pair_far: int32 [4, 4, 8, 32, 256], P('gx', 'gy', 'gz'), may hold values from 0 to 261, as said below
- far_line: int32 [4, 4, 8, 32], P('gx', 'gy', 'gz'), may hold values from 0 to 483, as said below
- pair_geom: float32 [4, 4, 8, 32, 4, 256], P('gx', 'gy', 'gz'), may hold values from -4 to 4
- live_blocks: int32 [4, 4, 8], P('gx', 'gy', 'gz'), may hold values from 8 to 32, as said below
Outputs:
- corrected: float32 [3, 64, 64, 2048], P(None, 'gx', 'gy', 'gz')
- sweep_history: float32 [2, 5], replicated
Inputs may be any that keep to these rules, and one draw needn't show every extreme that they name: `pair_far`: together with far_line: at most one of the three coordinates of node b lies outside the owner block's own nodes; node b lies inside the whole grid; in slots below 16 node b is one of the owner block's own nodes. `far_line`: together with pair_far, as stated there. `live_blocks`: some owner block has all 32 slots live.
All inputs are finite; a program needn't handle non-finite values.
Results may differ from a plain program's by a relative error of at most 0.0001.
Values sent between devices are 32-bit elements; how exact they have to be, the bound alone decides.
No kernel may reach another device: no remote copies, remote signals or barrier semaphores. Data moves between devices by JAX's collectives and lax.ppermute only.
A program may use at most 64 MiB of HBM per device.

v0:
```python
import math

import jax
import jax.numpy as jnp
from jax import lax
from jax.sharding import Mesh
from jax.sharding import PartitionSpec as P

RIM = 3
SWEEPS = 5
GZ = ("gz_0", "gz_1")
GX_GY_GZ = ("gx", "gy", "gz_0", "gz_1")


relax_factor = 0.9
highest = lax.Precision.HIGHEST


def extended(cells, sides, width):
    for axis, dim in sides:
        count = lax.axis_size(axis)
        ends = count - 1
        head = lax.slice_in_dim(cells, 0, width, axis=dim)
        tail = lax.slice_in_dim(cells, cells.shape[dim] - width, cells.shape[dim], axis=dim)
        cells = jnp.concatenate(
            [
                lax.ppermute(tail, axis, [(i, (i + 1) % count) for i in range(ends)]),
                cells,
                lax.ppermute(head, axis, [((i + 1) % count, i) for i in range(ends)]),
            ],
            axis=dim,
        )
    return cells


def one_axis_at_a_time(x, axes):
    for axis in axes:
        x = lax.psum(x, axis)
    return x


def with_halo(x, sides, width):
    edges = {}
    for axis, dim in sides:
        count, length = (lax.axis_size(axis), x.shape[dim])
        up = [(i, (i + 1) % count) for i in range(count - 1)]
        last = lax.slice_in_dim(x, length - width, length, axis=dim)
        first = lax.slice_in_dim(x, 0, width, axis=dim)
        edges[dim] = (
            lax.ppermute(last, axis, up),
            lax.ppermute(first, axis, [(b, a) for a, b in up]),
        )
    done = []
    for _, dim in sides:
        low, high = edges[dim]
        around = [(width, width) if d in done else (0, 0) for d in range(x.ndim)]
        x = jnp.concatenate([jnp.pad(low, around), x, jnp.pad(high, around)], axis=dim)
        done.append(dim)
    return x


def node_sums(contribs, within, line_index, line_length, count_lines):
    blocks = contribs.shape[0]
    group_size = math.gcd(16, blocks)
    row_count = contribs.shape[1]
    columns = lax.broadcasted_iota(jnp.int32, (1, 1, line_length), 2)
    line_ids = lax.broadcasted_iota(jnp.int32, (1, count_lines), 1)

    def node_add_group(turn_idx, running):
        first_block = turn_idx * group_size
        term_part = lax.dynamic_slice_in_dim(contribs, first_block, group_size, 0)
        node_part = lax.dynamic_slice_in_dim(within, first_block, group_size, 0)
        line_part = lax.dynamic_slice_in_dim(line_index, first_block, group_size, 0)
        one_hot = (node_part[:, :, None] == columns).astype(jnp.float32)
        window = jnp.einsum("bcp,bpn->bcn", term_part, one_hot, precision=highest)
        line_hot = (line_part[:, None] == line_ids).astype(jnp.float32)
        return running + jnp.einsum("bl,bcn->cln", line_hot, window, precision=highest)

    initial = jnp.zeros((row_count, count_lines, line_length), jnp.float32)
    return lax.fori_loop(0, blocks // group_size, node_add_group, initial)


def select_lines(line_hot, field_lines):
    return jnp.einsum("bl,cln->bcn", line_hot, field_lines, precision=highest)


def sweep_terms(
    near_lines, far_lines, within, far_pos, line_index, geometry, live_mask, count_lines
):
    blocks = within.shape[0]
    group_size = math.gcd(16, blocks)
    near_cols = lax.broadcasted_iota(jnp.int32, (1, 1, near_lines.shape[2]), 2)
    far_cols = lax.broadcasted_iota(jnp.int32, (1, 1, far_lines.shape[2]), 2)
    line_ids = lax.broadcasted_iota(jnp.int32, (1, count_lines), 1)

    def sweep_add_group(turn_idx, carry):
        running, energy_sum = carry
        near_hot = (within[:, :, None] == near_cols).astype(jnp.float32)
        far_hot = (far_pos[:, :, None] == far_cols).astype(jnp.float32)
        near_vals = jnp.einsum("bcn,bpn->bcp", near_lines, near_hot, precision=highest)
        far_vals = jnp.einsum("bcn,bpn->bcp", far_lines, far_hot, precision=highest)
        differ = near_vals - far_vals
        gap_value = (
            geometry[:, 0, :] * differ[:, 0, :]
            + geometry[:, 1, :] * differ[:, 1, :]
            + geometry[:, 2, :] * differ[:, 2, :]
            - geometry[:, 3, :]
        )
        depth_value = jnp.where(live_mask, jnp.maximum(-gap_value, 0.0), 0.0)
        contribs = depth_value[:, None, :] * geometry[:, 0:3, :]
        window = jnp.einsum("bcp,bpn->bcn", contribs, near_hot, precision=highest)
        line_hot = (line_index[:, None] == line_ids).astype(jnp.float32)
        running = running + jnp.einsum("bl,bcn->cln", line_hot, window, precision=highest)
        return (running, energy_sum + jnp.sum(depth_value * depth_value))

    initial = (
        jnp.zeros((3, count_lines, near_lines.shape[2]), jnp.float32),
        jnp.zeros((), jnp.float32),
    )
    return lax.fori_loop(0, blocks // group_size, sweep_add_group, initial)


def local(positions, pair_node, pair_line, pair_far, far_line, pair_geom, live_blocks):
    within = pair_node[0, 0, 0]
    line_index = pair_line[0, 0, 0]
    far_pos = pair_far[0, 0, 0]
    far_index = far_line[0, 0, 0]
    geometry = pair_geom[0, 0, 0]
    live_count = live_blocks[0, 0, 0]
    size_x = positions.shape[1]
    size_y = positions.shape[2]
    size_z = positions.shape[3]
    blocks = within.shape[0]
    pair_count = within.shape[1]
    inner_count = blocks // 2
    count_lines = size_x * size_y
    ext_lines = (size_x + 2 * RIM) * (size_y + 2 * RIM)
    ext_z = size_z + 2 * RIM
    devices = lax.axis_size("gx") * lax.axis_size("gy") * lax.axis_size(GZ)
    slot_count = blocks * pair_count
    live_mask = lax.broadcasted_iota(jnp.int32, (blocks, 1), 0) < live_count
    near_hot = (line_index[:, None] == lax.broadcasted_iota(jnp.int32, (1, count_lines), 1)).astype(
        jnp.float32
    )
    far_hot = (far_index[:, None] == lax.broadcasted_iota(jnp.int32, (1, ext_lines), 1)).astype(
        jnp.float32
    )
    live_ones = jnp.broadcast_to(
        jnp.where(live_mask, 1.0, 0.0).astype(jnp.float32), (blocks, pair_count)
    )
    counts = node_sums(live_ones[:, None, :], within, line_index, size_z, count_lines).reshape(
        size_x, size_y, size_z
    )
    widths = ((0, 0), (RIM, RIM), (RIM, RIM), (RIM, RIM))
    padded = extended(positions, (("gx", 1), ("gy", 2), (GZ, 3)), RIM)
    current = positions
    energies = []
    residuals = []
    for sweep_idx in range(SWEEPS):
        near_lines = select_lines(near_hot, current.reshape(3, count_lines, size_z))
        local_pad = jnp.pad(current, widths).reshape(3, ext_lines, ext_z)
        inner_far = select_lines(far_hot[:inner_count], local_pad)
        inner_total, inner_energy = sweep_terms(
            near_lines[:inner_count],
            inner_far,
            within[:inner_count],
            far_pos[:inner_count],
            line_index[:inner_count],
            geometry[:inner_count],
            live_mask[:inner_count],
            count_lines,
        )
        outer_far = select_lines(far_hot[inner_count:], padded.reshape(3, ext_lines, ext_z))
        outer_total, outer_energy = sweep_terms(
            near_lines[inner_count:],
            outer_far,
            within[inner_count:],
            far_pos[inner_count:],
            line_index[inner_count:],
            geometry[inner_count:],
            live_mask[inner_count:],
            count_lines,
        )
        node_total = inner_total + outer_total
        energy_local = inner_energy + outer_energy
        total_energy = one_axis_at_a_time(energy_local, GX_GY_GZ)
        scale_factor = 1.0 / (1.0 + total_energy / (slot_count * devices))
        correction = (
            relax_factor
            * scale_factor
            * node_total.reshape(3, size_x, size_y, size_z)
            / (1.0 + counts)
        )
        current = current + correction
        residual_local = jnp.sum(correction * correction)
        residuals.append(one_axis_at_a_time(residual_local, GX_GY_GZ))
        energies.append(total_energy)
        if sweep_idx + 1 < SWEEPS:
            padded = with_halo(current, (("gx", 1), ("gy", 2), (GZ, 3)), RIM)
    history = jnp.stack(
        [
            jnp.sqrt(1.0 + jnp.stack(energies) / slot_count),
            jnp.sqrt(1.0 + jnp.stack(residuals) / (size_x * size_y * size_z)),
        ]
    )
    return (current, history)


def solution(mesh):
    finer = Mesh(
        mesh.devices.reshape(mesh.shape["gx"], mesh.shape["gy"], 4, 2), ("gx", "gy", "gz_0", "gz_1")
    )
    placed = (
        P(None, "gx", "gy", GZ),
        P("gx", "gy", GZ, None, None),
        P("gx", "gy", GZ, None),
        P("gx", "gy", GZ, None, None),
        P("gx", "gy", GZ, None),
        P("gx", "gy", GZ, None, None, None),
        P("gx", "gy", GZ),
    )
    return jax.shard_map(
        local,
        mesh=finer,
        in_specs=placed,
        out_specs=(P(None, "gx", "gy", GZ), P()),
        check_vma=False,
    )
```

profile of v0, /device:TPU:1, one launch (start us, length us, event | category | flops | bytes accessed | tf_op | source)
XLA Modules:
  0.0 486.6 jit_solution(8755252132308115107)
XLA Ops:
  3.7 5.0 %collective-permute-start = (f32[3,3,16,256]{3,1,2,0:T(4,128)S(1)}, f32[3,3,16,256]{3,1,2,0:T(4,128)S(1)}, u32[]{:S(2)}, u32[]{:S(2)}) collective-permute-start(f32[3,3,16,256]{3,1,2,0:T(4,128)S(1)} %get-tuple-element.628), channel_id=1, source_target_pairs={{0,32},{32,64},{64,96},{1,33},{33,65},{65,97},{2,34},{34,66},{66,9... | collective-permute-start | bytes 442376 | tf_op jit(solution)/shard_map/ppermute | solution.py:27
  12.9 3.0 reshape.413
  23.3 4.2 while.9
  31.2 4.0 collective-permute-start.2
  35.2 2.8 fusion.32
  43.1 4.0 collective-permute-start.5
  48.8 3.2 collective-permute-start.4
  55.0 2.5 pad_maximum_fusion
  66.6 8.1 %psum.280 = f32[]{:T(128)} all-reduce(f32[]{:T(128)S(6)} %add.441), channel_id=1, replica_groups=mesh['gx'=4,'gy'=4,'gz_0'=4,'gz_1'=2] {'gx'}, use_global_device_ids=true, to_apply=%region_2.3 | all-reduce | flops 1 | bytes 8 | tf_op jit(solution)/shard_map/psum | solution.py:38
  75.3 10.6 %psum.281 = f32[]{:T(128)} all-reduce(f32[]{:T(128)} %psum.280), channel_id=1, replica_groups=mesh['gx'=4,'gy'=4,'gz_0'=4,'gz_1'=2] {'gy'}, use_global_device_ids=true, to_apply=%region_3.4 | all-reduce | flops 1 | bytes 8 | tf_op jit(solution)/shard_map/psum | solution.py:38
  86.0 7.8 %psum.282 = f32[]{:T(128)} all-reduce(f32[]{:T(128)} %psum.281), channel_id=1, replica_groups=mesh['gx'=4,'gy'=4,'gz_0'=4,'gz_1'=2] {'gz_0'}, use_global_device_ids=true, to_apply=%region_4.5 | all-reduce | flops 1 | bytes 8 | tf_op jit(solution)/shard_map/psum | solution.py:38
  94.7 11.5 %psum.283 = f32[]{:T(128)} all-reduce(f32[]{:T(128)} %psum.282), channel_id=1, replica_groups=mesh['gx'=4,'gy'=4,'gz_0'=4,'gz_1'=2] {'gz_1'}, use_global_device_ids=true, to_apply=%region_5.6 | all-reduce | flops 1 | bytes 8 | tf_op jit(solution)/shard_map/psum | solution.py:38
  113.6 4.0 collective-permute-start.7
  117.6 3.9 collective-permute-start.6
  125.3 4.4 collective-permute-start.8
  132.3 4.8 select_maximum_fusion.9
  137.1 3.0 reshape.416
  144.9 3.0 reshape.417
  154.2 8.4 %psum.284 = f32[]{:T(128)} all-reduce(f32[]{:T(128)S(6)} %add.451), channel_id=1, replica_groups=mesh['gx'=4,'gy'=4,'gz_0'=4,'gz_1'=2] {'gx'}, use_global_device_ids=true, to_apply=%region_10.11 | all-reduce | flops 1 | bytes 8 | tf_op jit(solution)/shard_map/psum | solution.py:38
  162.5 6.6 %psum.285 = f32[]{:T(128)} all-reduce(f32[]{:T(128)} %psum.284), channel_id=1, replica_groups=mesh['gx'=4,'gy'=4,'gz_0'=4,'gz_1'=2] {'gy'}, use_global_device_ids=true, to_apply=%region_11.12 | all-reduce | flops 1 | bytes 8 | tf_op jit(solution)/shard_map/psum | solution.py:38
  170.8 6.6 %psum.286 = f32[]{:T(128)} all-reduce(f32[]{:T(128)} %psum.285), channel_id=1, replica_groups=mesh['gx'=4,'gy'=4,'gz_0'=4,'gz_1'=2] {'gz_0'}, use_global_device_ids=true, to_apply=%region_12.13 | all-reduce | flops 1 | bytes 8 | tf_op jit(solution)/shard_map/psum | solution.py:38
  178.0 9.3 %psum.287 = f32[]{:T(128)} all-reduce(f32[]{:T(128)} %psum.286), channel_id=1, replica_groups=mesh['gx'=4,'gy'=4,'gz_0'=4,'gz_1'=2] {'gz_1'}, use_global_device_ids=true, to_apply=%region_13.14 | all-reduce | flops 1 | bytes 8 | tf_op jit(solution)/shard_map/psum | solution.py:38
  194.7 4.3 collective-permute-start.13
  198.9 3.6 collective-permute-start.12
  204.3 2.8 fusion.38
  207.1 4.2 collective-permute-start.14
  211.2 2.8 fusion.28
  214.3 4.4 select_maximum_fusion.6
  218.6 3.0 reshape.419
  229.4 2.5 fusion.255
  236.3 8.4 %psum.288 = f32[]{:T(128)} all-reduce(f32[]{:T(128)S(6)} %add.459), channel_id=1, replica_groups=mesh['gx'=4,'gy'=4,'gz_0'=4,'gz_1'=2] {'gx'}, use_global_device_ids=true, to_apply=%region_16.17 | all-reduce | flops 1 | bytes 8 | tf_op jit(solution)/shard_map/psum | solution.py:38
  244.7 8.0 %psum.289 = f32[]{:T(128)} all-reduce(f32[]{:T(128)} %psum.288), channel_id=1, replica_groups=mesh['gx'=4,'gy'=4,'gz_0'=4,'gz_1'=2] {'gy'}, use_global_device_ids=true, to_apply=%region_17.18 | all-reduce | flops 1 | bytes 8 | tf_op jit(solution)/shard_map/psum | solution.py:38
  254.4 8.6 %psum.290 = f32[]{:T(128)} all-reduce(f32[]{:T(128)} %psum.289), channel_id=1, replica_groups=mesh['gx'=4,'gy'=4,'gz_0'=4,'gz_1'=2] {'gz_0'}, use_global_device_ids=true, to_apply=%region_18.19 | all-reduce | flops 1 | bytes 8 | tf_op jit(solution)/shard_map/psum | solution.py:38
  263.5 9.0 %psum.291 = f32[]{:T(128)} all-reduce(f32[]{:T(128)} %psum.290), channel_id=1, replica_groups=mesh['gx'=4,'gy'=4,'gz_0'=4,'gz_1'=2] {'gz_1'}, use_global_device_ids=true, to_apply=%region_19.20 | all-reduce | flops 1 | bytes 8 | tf_op jit(solution)/shard_map/psum | solution.py:38
  280.0 4.0 collective-permute-start.19
  284.0 3.9 collective-permute-start.18
  291.8 4.2 collective-permute-start.20
  298.7 4.8 select_maximum_fusion.3
  303.5 3.0 reshape.422
  311.4 3.0 reshape.423
  320.4 8.4 %psum.292 = f32[]{:T(128)} all-reduce(f32[]{:T(128)S(6)} %add.467), channel_id=1, replica_groups=mesh['gx'=4,'gy'=4,'gz_0'=4,'gz_1'=2] {'gx'}, use_global_device_ids=true, to_apply=%region_22.23 | all-reduce | flops 1 | bytes 8 | tf_op jit(solution)/shard_map/psum | solution.py:38
  328.9 6.5 %psum.293 = f32[]{:T(128)} all-reduce(f32[]{:T(128)} %psum.292), channel_id=1, replica_groups=mesh['gx'=4,'gy'=4,'gz_0'=4,'gz_1'=2] {'gy'}, use_global_device_ids=true, to_apply=%region_23.24 | all-reduce | flops 1 | bytes 8 | tf_op jit(solution)/shard_map/psum | solution.py:38
  337.0 6.6 %psum.294 = f32[]{:T(128)} all-reduce(f32[]{:T(128)} %psum.293), channel_id=1, replica_groups=mesh['gx'=4,'gy'=4,'gz_0'=4,'gz_1'=2] {'gz_0'}, use_global_device_ids=true, to_apply=%region_24.25 | all-reduce | flops 1 | bytes 8 | tf_op jit(solution)/shard_map/psum | solution.py:38
  344.2 9.7 %psum.295 = f32[]{:T(128)} all-reduce(f32[]{:T(128)} %psum.294), channel_id=1, replica_groups=mesh['gx'=4,'gy'=4,'gz_0'=4,'gz_1'=2] {'gz_1'}, use_global_device_ids=true, to_apply=%region_25.26 | all-reduce | flops 1 | bytes 8 | tf_op jit(solution)/shard_map/psum | solution.py:38
  361.3 4.0 collective-permute-start.25
  365.3 3.9 collective-permute-start.24
  370.9 2.8 fusion.34
  373.7 4.2 collective-permute-start.26
  378.0 2.8 fusion.24
  380.8 4.4 select_maximum_fusion
  385.2 3.0 reshape.425
  388.2 2.5 fusion.248
  403.8 2.8 fusion.33
  406.6 8.3 %psum.296 = f32[]{:T(128)} all-reduce(f32[]{:T(128)S(6)} %add.475), channel_id=1, replica_groups=mesh['gx'=4,'gy'=4,'gz_0'=4,'gz_1'=2] {'gx'}, use_global_device_ids=true, to_apply=%region_28.29 | all-reduce | flops 1 | bytes 8 | tf_op jit(solution)/shard_map/psum | solution.py:38
  417.3 7.9 %psum.297 = f32[]{:T(128)} all-reduce(f32[]{:T(128)} %psum.296), channel_id=1, replica_groups=mesh['gx'=4,'gy'=4,'gz_0'=4,'gz_1'=2] {'gy'}, use_global_device_ids=true, to_apply=%region_29.30 | all-reduce | flops 1 | bytes 8 | tf_op jit(solution)/shard_map/psum | solution.py:38
  425.1 8.2 %psum.298 = f32[]{:T(128)} all-reduce(f32[]{:T(128)} %psum.297), channel_id=1, replica_groups=mesh['gx'=4,'gy'=4,'gz_0'=4,'gz_1'=2] {'gz_0'}, use_global_device_ids=true, to_apply=%region_30.31 | all-reduce | flops 1 | bytes 8 | tf_op jit(solution)/shard_map/psum | solution.py:38
  435.6 9.4 %psum.299 = f32[]{:T(128)} all-reduce(f32[]{:T(128)} %psum.298), channel_id=1, replica_groups=mesh['gx'=4,'gy'=4,'gz_0'=4,'gz_1'=2] {'gz_1'}, use_global_device_ids=true, to_apply=%region_31.32 | all-reduce | flops 1 | bytes 8 | tf_op jit(solution)/shard_map/psum | solution.py:38
  445.8 3.1 fusion.96
  449.9 6.8 %all-reduce.23 = (f32[]{:T(128)}, f32[]{:T(128)}, f32[]{:T(128)}, f32[]{:T(128)}, f32[]{:T(128)}) all-reduce(f32[]{:T(128)} %get-tuple-element.530, f32[]{:T(128)} %get-tuple-element.527, f32[]{:T(128)} %get-tuple-element.528, f32[]{:T(128)} %get-tuple-element.529, ...), channel_id=1, replica_groups=mesh['gx'=4,'gy'=4,'gz_0'=4,'gz_1'=2] {'gx'}, use_global_device_ids=true, to_apply=%region_33.34 | all-reduce | flops 5 | bytes 40 | tf_op jit(solution)/shard_map/psum | solution.py:38
  456.7 7.0 %all-reduce.22 = (f32[]{:T(128)}, f32[]{:T(128)}, f32[]{:T(128)}, f32[]{:T(128)}, f32[]{:T(128)}) all-reduce(f32[]{:T(128)} %get-tuple-element.564, f32[]{:T(128)} %get-tuple-element.565, f32[]{:T(128)} %get-tuple-element.566, f32[]{:T(128)} %get-tuple-element.567, ...), channel_id=1, replica_groups=mesh['gx'=4,'gy'=4,'gz_0'=4,'gz_1'=2] {'gy'}, use_global_device_ids=true, to_apply=%region_34.35 | all-reduce | flops 5 | bytes 40 | tf_op jit(solution)/shard_map/psum | solution.py:38
  463.7 6.7 %all-reduce.21 = (f32[]{:T(128)}, f32[]{:T(128)}, f32[]{:T(128)}, f32[]{:T(128)}, f32[]{:T(128)}) all-reduce(f32[]{:T(128)} %get-tuple-element.559, f32[]{:T(128)} %get-tuple-element.560, f32[]{:T(128)} %get-tuple-element.561, f32[]{:T(128)} %get-tuple-element.562, ...), channel_id=1, replica_groups=mesh['gx'=4,'gy'=4,'gz_0'=4,'gz_1'=2] {'gz_0'}, use_global_device_ids=true, to_apply=%region_35.36 | all-reduce | flops 5 | bytes 40 | tf_op jit(solution)/shard_map/psum | solution.py:38
  470.4 8.6 %all-reduce.24 = (f32[1,1]{1,0:T(1,128)}, f32[1,1]{1,0:T(1,128)}, f32[1,1]{1,0:T(1,128)}, f32[1,1]{1,0:T(1,128)}, f32[1,1]{1,0:T(1,128)}) all-reduce(f32[1,1]{1,0:T(1,128)} %bitcast.57, f32[1,1]{1,0:T(1,128)} %bitcast.58, f32[1,1]{1,0:T(1,128)} %bitcast.59, ...), channel_id=1, replica_groups=mesh['gx'=4,'gy'=4,'gz_0'=4,'gz_1'=2] {'gz_1'}, use_global_device_ids=true, to_apply=%region_36.37 | all-reduce | flops 5 | bytes 40 | tf_op jit(solution)/shard_map/psum | solution.py:38
  479.0 3.2 stack.52
  482.2 3.3 stack.46
  (304 shorter events, 138.7 us)
Async XLA Ops:
  0.6 10.2 %copy-start = (f32[3,16,16,256]{3,2,1,0:T(8,128)S(1)}, f32[3,16,16,256]{3,2,1,0:T(8,128)}, u32[]{:S(2)}) copy-start(f32[3,16,16,256]{3,2,1,0:T(8,128)} %param.9) | copy-start | bytes 2359300
  0.6 8.8 %copy-start.21 = (f32[1,1,1,32,4,256]{5,4,3,2,1,0:T(4,128)S(1)}, f32[1,1,1,32,4,256]{5,4,3,2,1,0:T(4,128)}, u32[]{:S(2)}) copy-start(f32[1,1,1,32,4,256]{5,4,3,2,1,0:T(4,128)} %param.14) | copy-start | bytes 393220
  0.6 9.6 %copy-start.30 = (s32[1,1,1,32,256]{4,3,2,1,0:T(8,128)S(1)}, s32[1,1,1,32,256]{4,3,2,1,0:T(8,128)}, u32[]{:S(2)}) copy-start(s32[1,1,1,32,256]{4,3,2,1,0:T(8,128)} %param.12) | copy-start | bytes 98308
  2.4 27.4 %collective-permute-start.1 = (f32[3,3,16,256]{3,1,2,0:T(4,128)S(1)}, f32[3,3,16,256]{3,1,2,0:T(4,128)S(1)}, u32[]{:S(2)}, u32[]{:S(2)}) collective-permute-start(f32[3,3,16,256]{3,1,2,0:T(4,128)S(1)} %get-tuple-element.629), channel_id=1, source_target_pairs={{32,0},{64,32},{96,64},{33,1},{65,33},{97,65},{34,2},{66,34},{98,6... | collective-permute-start | bytes 442376 | tf_op jit(solution)/shard_map/ppermute | solution.py:29
  3.7 26.1 %collective-permute-start = (f32[3,3,16,256]{3,1,2,0:T(4,128)S(1)}, f32[3,3,16,256]{3,1,2,0:T(4,128)S(1)}, u32[]{:S(2)}, u32[]{:S(2)}) collective-permute-start(f32[3,3,16,256]{3,1,2,0:T(4,128)S(1)} %get-tuple-element.628), channel_id=1, source_target_pairs={{0,32},{32,64},{64,96},{1,33},{33,65},{65,97},{2,34},{34,66},{66,9... | collective-permute-start | bytes 442376 | tf_op jit(solution)/shard_map/ppermute | solution.py:27
  9.5 18.1 %copy-start.39 = (s32[16,256]{1,0:T(8,128)}, s32[16,256]{1,0:T(8,128)S(1)}, u32[]{:S(2)}) copy-start(s32[16,256]{1,0:T(8,128)S(1)} %get-tuple-element.650) | copy-start | bytes 49156
  9.5 25.7 %copy-start.36 = (s32[16,256]{1,0:T(8,128)}, s32[16,256]{1,0:T(8,128)S(1)}, u32[]{:S(2)}) copy-start(s32[16,256]{1,0:T(8,128)S(1)} %get-tuple-element.649) | copy-start | bytes 49156
  10.8 8.1 %copy-start.47 = (s32[16,256]{1,0:T(8,128)}, s32[16,256]{1,0:T(8,128)S(1)}, u32[]{:S(2)}) copy-start(s32[16,256]{1,0:T(8,128)S(1)} %get-tuple-element.652) | copy-start | bytes 49156
  16.0 6.6 %copy-start.17 = (pred[32,484]{1,0:T(8,128)(4,1)}, pred[32,484]{1,0:T(8,128)(4,1)S(1)}, u32[]{:S(2)}) copy-start(pred[32,484]{1,0:T(8,128)(4,1)S(1)} %iota_compare_fusion.46) | copy-start | bytes 46468
  16.4 6.5 %copy-start.20 = (s32[1,1,1,32,256]{4,3,2,1,0:T(8,128)S(1)}, s32[1,1,1,32,256]{4,3,2,1,0:T(8,128)}, u32[]{:S(2)}) copy-start(s32[1,1,1,32,256]{4,3,2,1,0:T(8,128)} %param.10) | copy-start | bytes 98308
  29.8 8.2 %copy-start.13 = (f32[3,3,16,256]{3,1,2,0:T(4,128)}, f32[3,3,16,256]{3,1,2,0:T(4,128)S(1)}, u32[]{:S(2)}) copy-start(f32[3,3,16,256]{3,1,2,0:T(4,128)S(1)} %collective-permute-done.1) | copy-start | bytes 442372
  29.8 8.2 %copy-start.14 = (f32[3,3,16,256]{3,1,2,0:T(4,128)}, f32[3,3,16,256]{3,1,2,0:T(4,128)S(1)}, u32[]{:S(2)}) copy-start(f32[3,3,16,256]{3,1,2,0:T(4,128)S(1)} %collective-permute-done) | copy-start | bytes 442372
  29.9 8.1 %collective-permute-start.3 = (f32[3,22,3,256]{3,1,2,0:T(8,128)S(1)}, f32[3,22,3,256]{3,1,2,0:T(8,128)S(1)}, u32[]{:S(2)}, u32[]{:S(2)}) collective-permute-start(f32[3,22,3,256]{3,1,2,0:T(8,128)S(1)} %get-tuple-element.595), channel_id=1, source_target_pairs={{8,0},{16,8},{24,16},{9,1},{17,9},{25,17},{10,2},{18,10},{26,18},{... | collective-permute-start | bytes 608264 | tf_op jit(solution)/shard_map/ppermute | solution.py:29
  31.2 7.5 %collective-permute-start.2 = (f32[3,22,3,256]{3,1,2,0:T(8,128)S(1)}, f32[3,22,3,256]{3,1,2,0:T(8,128)S(1)}, u32[]{:S(2)}, u32[]{:S(2)}) collective-permute-start(f32[3,22,3,256]{3,1,2,0:T(8,128)S(1)} %get-tuple-element.594), channel_id=1, source_target_pairs={{0,8},{8,16},{16,24},{1,9},{9,17},{17,25},{2,10},{10,18},{18,26},{... | collective-permute-start | bytes 608264 | tf_op jit(solution)/shard_map/ppermute | solution.py:27
  43.1 9.6 %collective-permute-start.5 = (f32[3,22,22,3]{2,1,3,0:T(8,128)S(1)}, f32[3,22,22,3]{2,1,3,0:T(8,128)S(1)}, u32[]{:S(2)}, u32[]{:S(2)}) collective-permute-start(f32[3,22,22,3]{2,1,3,0:T(8,128)S(1)} %copy.135), channel_id=1, source_target_pairs={{1,0},{2,1},{3,2},{4,3},{5,4},{6,5},{7,6},{9,8},{10,9},{11,10},{12... | collective-permute-start | bytes 52280 | tf_op jit(solution)/shard_map/ppermute | solution.py:29
  48.8 4.8 collective-permute-start.4
  59.7 6.9 %copy-start.32 = (s32[1,1,1,32]{3,2,1,0:T(1,128)S(1)}, s32[1,1,1,32]{3,2,1,0:T(1,128)}, u32[]{:S(2)}) copy-start(s32[1,1,1,32]{3,2,1,0:T(1,128)} %param.11) | copy-start | bytes 388
  59.7 15.1 %copy-start.29 = (f32[16,3,256]{2,1,0:T(4,128)S(1)}, f32[16,3,256]{2,1,0:T(4,128)}, u32[]{:S(2)}) copy-start(f32[16,3,256]{2,1,0:T(4,128)} %fusion.41) | copy-start | bytes 147460
  62.2 44.7 %copy-start.37 = (s32[16,256]{1,0:T(8,128)S(1)}, s32[16,256]{1,0:T(8,128)}, u32[]{:S(2)}) copy-start(s32[16,256]{1,0:T(8,128)} %copy-done.36) | copy-start | bytes 49156
  66.6 42.4 %copy-start.50 = (s32[16]{0:T(128)}, s32[16]{0:T(128)S(1)}, u32[]{:S(2)}) copy-start(s32[16]{0:T(128)S(1)} %get-tuple-element.655) | copy-start | bytes 196
  66.6 110.7 %copy-start.34 = (s32[16]{0:T(128)}, s32[16]{0:T(128)S(1)}, u32[]{:S(2)}) copy-start(s32[16]{0:T(128)S(1)} %get-tuple-element.656) | copy-start | bytes 196
  109.3 13.9 %copy-start.40 = (s32[16,256]{1,0:T(8,128)S(1)}, s32[16,256]{1,0:T(8,128)}, u32[]{:S(2)}) copy-start(s32[16,256]{1,0:T(8,128)} %copy-done.39) | copy-start | bytes 49156
  110.0 15.3 %collective-permute-start.11 = (f32[3,16,16,3]{3,2,1,0:T(8,128)S(1)}, f32[3,16,16,3]{3,2,1,0:T(8,128)S(1)}, u32[]{:S(2)}, u32[]{:S(2)}) collective-permute-start(f32[3,16,16,3]{3,2,1,0:T(8,128)S(1)} %get-tuple-element.625), channel_id=1, source_target_pairs={{1,0},{2,1},{3,2},{4,3},{5,4},{6,5},{7,6},{9,8},{10,9},{11,10},{12... | collective-permute-start | bytes 27656 | tf_op jit(solution)/shard_map/ppermute | solution.py:51
  112.3 19.6 %collective-permute-start.10 = (f32[3,16,3,256]{3,2,1,0:T(4,128)S(1)}, f32[3,16,3,256]{3,2,1,0:T(4,128)S(1)}, u32[]{:S(2)}, u32[]{:S(2)}) collective-permute-start(f32[3,16,3,256]{3,2,1,0:T(4,128)S(1)} %get-tuple-element.627), channel_id=1, source_target_pairs={{8,0},{16,8},{24,16},{9,1},{17,9},{25,17},{10,2},{18,10},{26,18},{... | collective-permute-start | bytes 442376 | tf_op jit(solution)/shard_map/ppermute | solution.py:51
  113.6 18.4 %collective-permute-start.7 = (f32[3,16,3,256]{3,2,1,0:T(4,128)S(1)}, f32[3,16,3,256]{3,2,1,0:T(4,128)S(1)}, u32[]{:S(2)}, u32[]{:S(2)}) collective-permute-start(f32[3,16,3,256]{3,2,1,0:T(4,128)S(1)} %get-tuple-element.626), channel_id=1, source_target_pairs={{0,8},{8,16},{16,24},{1,9},{9,17},{17,25},{2,10},{10,18},{18,26},{... | collective-permute-start | bytes 442376 | tf_op jit(solution)/shard_map/ppermute | solution.py:50
  117.6 14.3 %collective-permute-start.6 = (f32[3,16,16,3]{3,2,1,0:T(8,128)S(1)}, f32[3,16,16,3]{3,2,1,0:T(8,128)S(1)}, u32[]{:S(2)}, u32[]{:S(2)}) collective-permute-start(f32[3,16,16,3]{3,2,1,0:T(8,128)S(1)} %get-tuple-element.624), channel_id=1, source_target_pairs={{0,1},{1,2},{2,3},{3,4},{4,5},{5,6},{6,7},{8,9},{9,10},{10,11},{11... | collective-permute-start | bytes 27656 | tf_op jit(solution)/shard_map/ppermute | solution.py:50
  121.4 10.5 %collective-permute-start.9 = (f32[3,3,16,256]{3,2,1,0:T(8,128)S(1)}, f32[3,3,16,256]{3,2,1,0:T(8,128)S(1)}, u32[]{:S(2)}, u32[]{:S(2)}) collective-permute-start(f32[3,3,16,256]{3,2,1,0:T(8,128)S(1)} %get-tuple-element.623), channel_id=1, source_target_pairs={{32,0},{64,32},{96,64},{33,1},{65,33},{97,65},{34,2},{66,34},{98,6... | collective-permute-start | bytes 442376 | tf_op jit(solution)/shard_map/ppermute | solution.py:51
  125.3 7.0 %collective-permute-start.8 = (f32[3,3,16,256]{3,2,1,0:T(8,128)S(1)}, f32[3,3,16,256]{3,2,1,0:T(8,128)S(1)}, u32[]{:S(2)}, u32[]{:S(2)}) collective-permute-start(f32[3,3,16,256]{3,2,1,0:T(8,128)S(1)} %get-tuple-element.622), channel_id=1, source_target_pairs={{0,32},{32,64},{64,96},{1,33},{33,65},{65,97},{2,34},{34,66},{66,9... | collective-permute-start | bytes 442376 | tf_op jit(solution)/shard_map/ppermute | solution.py:50
  137.1 5.6 %copy-start.48 = (s32[16,256]{1,0:T(8,128)S(1)}, s32[16,256]{1,0:T(8,128)}, u32[]{:S(2)}) copy-start(s32[16,256]{1,0:T(8,128)} %copy-done.47) | copy-start | bytes 49156
  144.9 5.5 %copy-start.45 = (s32[16,256]{1,0:T(8,128)S(1)}, s32[16,256]{1,0:T(8,128)}, u32[]{:S(2)}) copy-start(s32[16,256]{1,0:T(8,128)} %get-tuple-element.651) | copy-start | bytes 49156
  150.4 39.2 %copy-start.51 = (s32[16]{0:T(128)S(1)}, s32[16]{0:T(128)}, u32[]{:S(2)}) copy-start(s32[16]{0:T(128)} %copy-done.50) | copy-start | bytes 196
  190.4 13.9 %copy-start.41 = (s32[16,256]{1,0:T(8,128)S(1)}, s32[16,256]{1,0:T(8,128)}, u32[]{:S(2)}) copy-start(s32[16,256]{1,0:T(8,128)} %copy-done.39) | copy-start | bytes 49156
  191.1 16.0 %collective-permute-start.17 = (f32[3,16,16,3]{3,2,1,0:T(8,128)S(1)}, f32[3,16,16,3]{3,2,1,0:T(8,128)S(1)}, u32[]{:S(2)}, u32[]{:S(2)}) collective-permute-start(f32[3,16,16,3]{3,2,1,0:T(8,128)S(1)} %get-tuple-element.617), channel_id=1, source_target_pairs={{1,0},{2,1},{3,2},{4,3},{5,4},{6,5},{7,6},{9,8},{10,9},{11,10},{12... | collective-permute-start | bytes 27656 | tf_op jit(solution)/shard_map/ppermute | solution.py:51
  193.4 20.6 %collective-permute-start.16 = (f32[3,16,3,256]{3,2,1,0:T(4,128)S(1)}, f32[3,16,3,256]{3,2,1,0:T(4,128)S(1)}, u32[]{:S(2)}, u32[]{:S(2)}) collective-permute-start(f32[3,16,3,256]{3,2,1,0:T(4,128)S(1)} %get-tuple-element.619), channel_id=1, source_target_pairs={{8,0},{16,8},{24,16},{9,1},{17,9},{25,17},{10,2},{18,10},{26,18},{... | collective-permute-start | bytes 442376 | tf_op jit(solution)/shard_map/ppermute | solution.py:51
  194.7 19.4 %collective-permute-start.13 = (f32[3,16,3,256]{3,2,1,0:T(4,128)S(1)}, f32[3,16,3,256]{3,2,1,0:T(4,128)S(1)}, u32[]{:S(2)}, u32[]{:S(2)}) collective-permute-start(f32[3,16,3,256]{3,2,1,0:T(4,128)S(1)} %get-tuple-element.618), channel_id=1, source_target_pairs={{0,8},{8,16},{16,24},{1,9},{9,17},{17,25},{2,10},{10,18},{18,26},{... | collective-permute-start | bytes 442376 | tf_op jit(solution)/shard_map/ppermute | solution.py:50
  198.9 15.1 %collective-permute-start.12 = (f32[3,16,16,3]{3,2,1,0:T(8,128)S(1)}, f32[3,16,16,3]{3,2,1,0:T(8,128)S(1)}, u32[]{:S(2)}, u32[]{:S(2)}) collective-permute-start(f32[3,16,16,3]{3,2,1,0:T(8,128)S(1)} %get-tuple-element.616), channel_id=1, source_target_pairs={{0,1},{1,2},{2,3},{3,4},{4,5},{5,6},{6,7},{8,9},{9,10},{10,11},{11... | collective-permute-start | bytes 27656 | tf_op jit(solution)/shard_map/ppermute | solution.py:50
  202.5 11.5 %collective-permute-start.15 = (f32[3,3,16,256]{3,2,1,0:T(8,128)S(1)}, f32[3,3,16,256]{3,2,1,0:T(8,128)S(1)}, u32[]{:S(2)}, u32[]{:S(2)}) collective-permute-start(f32[3,3,16,256]{3,2,1,0:T(8,128)S(1)} %get-tuple-element.615), channel_id=1, source_target_pairs={{32,0},{64,32},{96,64},{33,1},{65,33},{97,65},{34,2},{66,34},{98,6... | collective-permute-start | bytes 442376 | tf_op jit(solution)/shard_map/ppermute | solution.py:51
  207.1 7.2 %collective-permute-start.14 = (f32[3,3,16,256]{3,2,1,0:T(8,128)S(1)}, f32[3,3,16,256]{3,2,1,0:T(8,128)S(1)}, u32[]{:S(2)}, u32[]{:S(2)}) collective-permute-start(f32[3,3,16,256]{3,2,1,0:T(8,128)S(1)} %get-tuple-element.614), channel_id=1, source_target_pairs={{0,32},{32,64},{64,96},{1,33},{33,65},{65,97},{2,34},{34,66},{66,9... | collective-permute-start | bytes 442376 | tf_op jit(solution)/shard_map/ppermute | solution.py:50
  229.4 6.8 %copy-start.28 = (f32[16,1,256]{2,0,1:T(8,128)S(1)}, f32[16,1,256]{2,0,1:T(8,128)}, u32[]{:S(2)}) copy-start(f32[16,1,256]{2,0,1:T(8,128)} %get-tuple-element.583) | copy-start | bytes 49156
  229.4 15.4 %copy-start.4 = (f32[16,4,256]{2,0,1:T(8,128)S(1)}, f32[16,4,256]{2,0,1:T(8,128)}, u32[]{:S(2)}) copy-start(f32[16,4,256]{2,0,1:T(8,128)} %copy-done.1) | copy-start | bytes 196612
  229.4 23.4 %copy-start.42 = (s32[16,256]{1,0:T(8,128)S(1)}, s32[16,256]{1,0:T(8,128)}, u32[]{:S(2)}) copy-start(s32[16,256]{1,0:T(8,128)} %copy-done.39) | copy-start | bytes 49156
  229.4 33.6 %copy-start.35 = (s32[16]{0:T(128)S(1)}, s32[16]{0:T(128)}, u32[]{:S(2)}) copy-start(s32[16]{0:T(128)} %copy-done.34) | copy-start | bytes 196
  231.9 41.3 %copy-start.38 = (s32[16,256]{1,0:T(8,128)S(1)}, s32[16,256]{1,0:T(8,128)}, u32[]{:S(2)}) copy-start(s32[16,256]{1,0:T(8,128)} %copy-done.36) | copy-start | bytes 49156
  231.9 42.9 %copy-start.52 = (s32[16]{0:T(128)S(1)}, s32[16]{0:T(128)}, u32[]{:S(2)}) copy-start(s32[16]{0:T(128)} %copy-done.50) | copy-start | bytes 196
  275.4 13.7 %copy-start.33 = (s32[1,1,1,32]{3,2,1,0:T(1,128)S(1)}, s32[1,1,1,32]{3,2,1,0:T(1,128)}, u32[]{:S(2)}) copy-start(s32[1,1,1,32]{3,2,1,0:T(1,128)} %param.11) | copy-start | bytes 388
  275.7 13.9 %copy-start.43 = (s32[16,256]{1,0:T(8,128)S(1)}, s32[16,256]{1,0:T(8,128)}, u32[]{:S(2)}) copy-start(s32[16,256]{1,0:T(8,128)} %copy-done.39) | copy-start | bytes 49156
  276.4 15.3 %collective-permute-start.23 = (f32[3,16,16,3]{3,2,1,0:T(8,128)S(1)}, f32[3,16,16,3]{3,2,1,0:T(8,128)S(1)}, u32[]{:S(2)}, u32[]{:S(2)}) collective-permute-start(f32[3,16,16,3]{3,2,1,0:T(8,128)S(1)} %get-tuple-element.609), channel_id=1, source_target_pairs={{1,0},{2,1},{3,2},{4,3},{5,4},{6,5},{7,6},{9,8},{10,9},{11,10},{12... | collective-permute-start | bytes 27656 | tf_op jit(solution)/shard_map/ppermute | solution.py:51
  278.7 19.5 %collective-permute-start.22 = (f32[3,16,3,256]{3,2,1,0:T(4,128)S(1)}, f32[3,16,3,256]{3,2,1,0:T(4,128)S(1)}, u32[]{:S(2)}, u32[]{:S(2)}) collective-permute-start(f32[3,16,3,256]{3,2,1,0:T(4,128)S(1)} %get-tuple-element.611), channel_id=1, source_target_pairs={{8,0},{16,8},{24,16},{9,1},{17,9},{25,17},{10,2},{18,10},{26,18},{... | collective-permute-start | bytes 442376 | tf_op jit(solution)/shard_map/ppermute | solution.py:51
  280.0 18.2 %collective-permute-start.19 = (f32[3,16,3,256]{3,2,1,0:T(4,128)S(1)}, f32[3,16,3,256]{3,2,1,0:T(4,128)S(1)}, u32[]{:S(2)}, u32[]{:S(2)}) collective-permute-start(f32[3,16,3,256]{3,2,1,0:T(4,128)S(1)} %get-tuple-element.610), channel_id=1, source_target_pairs={{0,8},{8,16},{16,24},{1,9},{9,17},{17,25},{2,10},{10,18},{18,26},{... | collective-permute-start | bytes 442376 | tf_op jit(solution)/shard_map/ppermute | solution.py:50
  284.0 14.1 %collective-permute-start.18 = (f32[3,16,16,3]{3,2,1,0:T(8,128)S(1)}, f32[3,16,16,3]{3,2,1,0:T(8,128)S(1)}, u32[]{:S(2)}, u32[]{:S(2)}) collective-permute-start(f32[3,16,16,3]{3,2,1,0:T(8,128)S(1)} %get-tuple-element.608), channel_id=1, source_target_pairs={{0,1},{1,2},{2,3},{3,4},{4,5},{5,6},{6,7},{8,9},{9,10},{10,11},{11... | collective-permute-start | bytes 27656 | tf_op jit(solution)/shard_map/ppermute | solution.py:50
  287.9 10.3 %collective-permute-start.21 = (f32[3,3,16,256]{3,2,1,0:T(8,128)S(1)}, f32[3,3,16,256]{3,2,1,0:T(8,128)S(1)}, u32[]{:S(2)}, u32[]{:S(2)}) collective-permute-start(f32[3,3,16,256]{3,2,1,0:T(8,128)S(1)} %get-tuple-element.607), channel_id=1, source_target_pairs={{32,0},{64,32},{96,64},{33,1},{65,33},{97,65},{34,2},{66,34},{98,6... | collective-permute-start | bytes 442376 | tf_op jit(solution)/shard_map/ppermute | solution.py:51
  291.8 7.0 %collective-permute-start.20 = (f32[3,3,16,256]{3,2,1,0:T(8,128)S(1)}, f32[3,3,16,256]{3,2,1,0:T(8,128)S(1)}, u32[]{:S(2)}, u32[]{:S(2)}) collective-permute-start(f32[3,3,16,256]{3,2,1,0:T(8,128)S(1)} %get-tuple-element.606), channel_id=1, source_target_pairs={{0,32},{32,64},{64,96},{1,33},{33,65},{65,97},{2,34},{34,66},{66,9... | collective-permute-start | bytes 442376 | tf_op jit(solution)/shard_map/ppermute | solution.py:50
  303.5 5.5 %copy-start.49 = (s32[16,256]{1,0:T(8,128)S(1)}, s32[16,256]{1,0:T(8,128)}, u32[]{:S(2)}) copy-start(s32[16,256]{1,0:T(8,128)} %copy-done.47) | copy-start | bytes 49156
  357.0 13.9 %copy-start.44 = (s32[16,256]{1,0:T(8,128)S(1)}, s32[16,256]{1,0:T(8,128)}, u32[]{:S(2)}) copy-start(s32[16,256]{1,0:T(8,128)} %copy-done.39) | copy-start | bytes 49156
  357.8 16.0 %collective-permute-start.29 = (f32[3,16,16,3]{3,2,1,0:T(8,128)S(1)}, f32[3,16,16,3]{3,2,1,0:T(8,128)S(1)}, u32[]{:S(2)}, u32[]{:S(2)}) collective-permute-start(f32[3,16,16,3]{3,2,1,0:T(8,128)S(1)} %get-tuple-element.601), channel_id=1, source_target_pairs={{1,0},{2,1},{3,2},{4,3},{5,4},{6,5},{7,6},{9,8},{10,9},{11,10},{12... | collective-permute-start | bytes 27656 | tf_op jit(solution)/shard_map/ppermute | solution.py:51
  360.0 20.7 %collective-permute-start.28 = (f32[3,16,3,256]{3,2,1,0:T(4,128)S(1)}, f32[3,16,3,256]{3,2,1,0:T(4,128)S(1)}, u32[]{:S(2)}, u32[]{:S(2)}) collective-permute-start(f32[3,16,3,256]{3,2,1,0:T(4,128)S(1)} %get-tuple-element.603), channel_id=1, source_target_pairs={{8,0},{16,8},{24,16},{9,1},{17,9},{25,17},{10,2},{18,10},{26,18},{... | collective-permute-start | bytes 442376 | tf_op jit(solution)/shard_map/ppermute | solution.py:51
  361.3 19.4 %collective-permute-start.25 = (f32[3,16,3,256]{3,2,1,0:T(4,128)S(1)}, f32[3,16,3,256]{3,2,1,0:T(4,128)S(1)}, u32[]{:S(2)}, u32[]{:S(2)}) collective-permute-start(f32[3,16,3,256]{3,2,1,0:T(4,128)S(1)} %get-tuple-element.602), channel_id=1, source_target_pairs={{0,8},{8,16},{16,24},{1,9},{9,17},{17,25},{2,10},{10,18},{18,26},{... | collective-permute-start | bytes 442376 | tf_op jit(solution)/shard_map/ppermute | solution.py:50
  365.3 15.4 %collective-permute-start.24 = (f32[3,16,16,3]{3,2,1,0:T(8,128)S(1)}, f32[3,16,16,3]{3,2,1,0:T(8,128)S(1)}, u32[]{:S(2)}, u32[]{:S(2)}) collective-permute-start(f32[3,16,16,3]{3,2,1,0:T(8,128)S(1)} %get-tuple-element.600), channel_id=1, source_target_pairs={{0,1},{1,2},{2,3},{3,4},{4,5},{5,6},{6,7},{8,9},{9,10},{10,11},{11... | collective-permute-start | bytes 27656 | tf_op jit(solution)/shard_map/ppermute | solution.py:50
  369.2 11.6 %collective-permute-start.27 = (f32[3,3,16,256]{3,2,1,0:T(8,128)S(1)}, f32[3,3,16,256]{3,2,1,0:T(8,128)S(1)}, u32[]{:S(2)}, u32[]{:S(2)}) collective-permute-start(f32[3,3,16,256]{3,2,1,0:T(8,128)S(1)} %get-tuple-element.599), channel_id=1, source_target_pairs={{32,0},{64,32},{96,64},{33,1},{65,33},{97,65},{34,2},{66,34},{98,6... | collective-permute-start | bytes 442376 | tf_op jit(solution)/shard_map/ppermute | solution.py:51
  373.7 7.0 %collective-permute-start.26 = (f32[3,3,16,256]{3,2,1,0:T(8,128)S(1)}, f32[3,3,16,256]{3,2,1,0:T(8,128)S(1)}, u32[]{:S(2)}, u32[]{:S(2)}) collective-permute-start(f32[3,3,16,256]{3,2,1,0:T(8,128)S(1)} %get-tuple-element.598), channel_id=1, source_target_pairs={{0,32},{32,64},{64,96},{1,33},{33,65},{65,97},{2,34},{34,66},{66,9... | collective-permute-start | bytes 442376 | tf_op jit(solution)/shard_map/ppermute | solution.py:50
  398.5 47.3 %copy-start.7 = (f32[3,256,256]{1,2,0:T(8,128)S(1)}, f32[3,256,256]{1,2,0:T(8,128)}, u32[]{:S(2)}) copy-start(f32[3,256,256]{1,2,0:T(8,128)} %copy-done.6) | copy-start | bytes 2359300
  398.5 47.3 %copy-start.9 = (f32[3,256,256]{1,2,0:T(8,128)S(1)}, f32[3,256,256]{1,2,0:T(8,128)}, u32[]{:S(2)}) copy-start(f32[3,256,256]{1,2,0:T(8,128)} %copy-done.8) | copy-start | bytes 2359300
  398.5 47.3 %copy-start.11 = (f32[3,256,256]{1,2,0:T(8,128)S(1)}, f32[3,256,256]{1,2,0:T(8,128)}, u32[]{:S(2)}) copy-start(f32[3,256,256]{1,2,0:T(8,128)} %copy-done.10) | copy-start | bytes 2359300
  400.9 44.9 %copy-start.53 = (s32[16]{0:T(128)S(1)}, s32[16]{0:T(128)}, u32[]{:S(2)}) copy-start(s32[16]{0:T(128)} %copy-done.50) | copy-start | bytes 196
  (21 other events, 71.3 us)
where the time goes:
time: 496 us; the launch traced here: 487 us
  blocking collectives  197 us (40%)
  matrix products  104 us (21%)
  starting transfers between devices  86.6 us (17%)
  local copies, waits for them, and re-layouts  48.9 us (10%)
  other arithmetic  35.3 us (7%)
  between operations  12.6 us (3%)
    psum x24, blocking collectives, one_axis_at_a_time(): x = lax.psum(x, axis)  197 us
    ppermute x12, starting transfers between devices, with_halo(): lax.ppermute(last, axis, up)  48.5 us
    dot_general x15, matrix products, select_lines(): return jnp.einsum('bl,cln->bcn', line_hot, field_lines, precision=highest)  27.1 us
    dot_general x10, matrix products, sweep_add_group(): jnp.einsum('bcn,bpn->bcp', near_lines, near_hot, precision=highest)  24.6 us
    ppermute x12, starting transfers between devices, with_halo(): lax.ppermute(first, axis, [(b, a) for a, b in up])  19.3 us
    dot_general x10, matrix products, sweep_add_group(): far_vals = jnp.einsum('bcn,bpn->bcp', far_lines, far_hot, precision=highest)  19.3 us
    dot_general x10, matrix products, sweep_add_group(): window = jnp.einsum('bcp,bpn->bcn', contribs, near_hot, precision=highest)  18.6 us
    concatenate x4, other arithmetic, with_halo(): jnp.concatenate([jnp.pad(low, around), x, jnp.pad(high, around)], axis=dim)  18.4 us
  transfers between devices with their start and end apart: 30, of which 5 were waited for; matrix products, arithmetic and copies ran while one was open for 10% of the time, Pallas kernels for 0%

commit v1 on v0

v1 whole, which is shorter than its diff:
```python
import functools

import jax
import jax.numpy as jnp
from jax import lax
from jax.experimental import pallas as pl
from jax.experimental.pallas import tpu as pltpu
from jax.sharding import Mesh
from jax.sharding import PartitionSpec as P

SWEEPS = 5
RELAX = 0.9
XY = ("gx", "gy")
GZ = ("gz_0", "gz_1")
ALL = ("gx", "gy", "gz_0", "gz_1")
F32 = jnp.float32
BF16 = jnp.bfloat16
I32 = jnp.int32
SLOTS = 32
OUTER = 16
N_PAIRS = 1048576
NODES_BLK = 65536
PAIRS_SLOTS = 8192


def iota(shape, dim):
    return lax.broadcasted_iota(I32, shape, dim)


def split3(x):
    hi = x.astype(BF16)
    rest = x - hi.astype(F32)
    mid = rest.astype(BF16)
    low = (rest - mid.astype(F32)).astype(BF16)
    return hi, mid, low


def pick(sel, x):
    hi, mid, low = split3(x)
    dot = functools.partial(jnp.dot, preferred_element_type=F32)
    return (dot(sel, low) + dot(sel, mid)) + dot(sel, hi)


def hot(a, b):
    return jnp.where(a == b, 1.0, 0.0).astype(BF16)


def column(row, first, count):
    shape = (count, row.shape[1])
    chosen = iota(shape, 0) + first == iota(shape, 1)
    return jnp.sum(jnp.where(chosen, jnp.broadcast_to(row, shape), 0.0), axis=1, keepdims=True)


def take128(x, index):
    return jnp.take_along_axis(x, index, axis=1, mode="promise_in_bounds")


def take_lanes(x, index):
    low = index & 127
    high = index >= 128
    parts = []
    for t in (0, 1):
        cut = slice(t * 128, (t + 1) * 128)
        a = take128(x[:, :128], low[:, cut])
        b = take128(x[:, 128:], low[:, cut])
        parts.append(jnp.where(high[:, cut], b, a))
    return jnp.concatenate(parts, axis=1)


def decode(far_line):
    x = (far_line * 2979) >> 16
    y = far_line - 22 * x - 3
    x = x - 3
    return x, y, (x & 15) * 16 + (y & 15)


def edge_lanes(parts, low_first, high_first):
    lane = iota((parts[0].shape[0], 128), 1)
    out = jnp.zeros((parts[0].shape[0], 128), F32)
    for c in range(3):
        for first, half, at in ((low_first, 0, 0), (high_first, 1, 125)):
            if first is None:
                continue
            to = first + 3 * c
            moved = parts[c][:, half * 128 : half * 128 + 128]
            if (to - at) % 128:
                moved = pltpu.roll(moved, (to - at) % 128, axis=1)
            out = jnp.where((lane >= to) & (lane < to + 3), moved, out)
    return out


def pack_kernel(pos, far, geom, fline, pline, xdn, xup, ydn, yup, zdn, zup, geom_out):
    for c in range(4):
        geom_out[c] = geom[:, c, :]
    fcol = column(fline[...].astype(F32), OUTER, OUTER).astype(I32)
    x, y, line = decode(fcol)
    tag = (line + 1).astype(F32)
    far_z = jnp.clip(far[OUTER:, :] - 3, 0, 255).astype(F32)
    for buf, mask in ((xdn, x < 0), (xup, x > 15), (ydn, y < 0), (yup, y > 15)):
        for c in range(3):
            buf[144 + 16 * c : 160 + 16 * c, :] = geom_out[c, OUTER:, :]
        buf[192:208, :] = far_z
        buf[208:224, :] = jnp.broadcast_to(jnp.where(mask, tag, 0.0), (OUTER, 256))
    for c in range(3):
        xdn[48 * c : 48 * c + 48, :] = pos[c, 0:48, :]
        xup[48 * c : 48 * c + 48, :] = pos[c, 208:256, :]
        for i in range(16):
            to = 48 * c + 3 * i
            ydn[to : to + 3, :] = pos[c, 16 * i : 16 * i + 3, :]
            yup[to : to + 3, :] = pos[c, 16 * i + 13 : 16 * i + 16, :]
    parts = [pos[c] for c in range(3)]
    zdn[0:256, :] = edge_lanes(parts, 0, None)
    zup[0:256, :] = edge_lanes(parts, None, 9)
    lines = jnp.broadcast_to(pline[...].astype(F32) + 1.0, (8, SLOTS))
    for buf in (zdn, zup):
        buf[256:264, :] = jnp.zeros((8, 128), F32)
        buf[256:264, 0:SLOTS] = lines


def z_index(far_outer):
    z = far_outer - 3
    below = z < 0
    above = z > 255
    index = jnp.where(below, z + 12, jnp.where(above, z - 256, 0))
    return index, below | above


def z_values(edges, far_outer):
    index, outside = z_index(far_outer)
    out = []
    for c in range(3):
        parts = [
            take128(edges, index[:, t * 128 : (t + 1) * 128] + 3 * c) for t in (0, 1)
        ]
        out.append(jnp.where(outside, jnp.concatenate(parts, axis=1), 0.0))
    return out


def scatter(rows, node, xs, ys):
    for r, value in enumerate(rows):
        for t in (0, 1):
            xs[t, pl.ds(r, SLOTS, stride=8), :] = value[:, t * 128 : (t + 1) * 128]
    for t in (0, 1):
        xs[t, pl.ds(4, SLOTS, stride=8), :] = node[:, t * 128 : (t + 1) * 128].astype(F32)
        for r in [r for r in range(len(rows), 8) if r != 4]:
            xs[t, pl.ds(r, SLOTS, stride=8), :] = jnp.zeros((SLOTS, 128), F32)
    places = iota((256, 256), 0).astype(F32).astype(BF16)
    one = jnp.ones((), BF16)
    zero = jnp.zeros((), BF16)

    def group(g, carry):
        for i in range(8):
            at = pl.multiple_of(g * 64 + i * 8, 8)
            x = jnp.concatenate([xs[0, pl.ds(at, 8), :], xs[1, pl.ds(at, 8), :]], axis=1)
            index = jnp.broadcast_to(x[4:5, :].astype(BF16), (256, 256))
            onehot = jnp.where(places == index, one, zero)
            hi = x.astype(BF16).astype(F32)
            rest = x - hi
            mid = rest.astype(BF16).astype(F32)
            lhs = jnp.concatenate([hi, mid, rest - mid, jnp.zeros_like(x)], axis=0).astype(BF16)
            got = lax.dot_general(
                lhs, onehot, (((1,), (1,)), ((), ())), preferred_element_type=F32
            )
            total = (got[16:24] + got[8:16]) + got[0:8]
            ys[0, pl.ds(at, 8), :] = total[:, :128]
            ys[1, pl.ds(at, 8), :] = total[:, 128:]
        return carry

    lax.fori_loop(0, SLOTS // 8, group, 0)
    return [
        jnp.concatenate([ys[t, pl.ds(r, SLOTS, stride=8), :] for t in (0, 1)], axis=1)
        for r in range(len(rows))
    ]


def pair_tile(first, second):
    lane = iota((8, 128), 1)
    return jnp.where(lane == 0, first, jnp.where(lane == 1, second, 0.0))


def depth_of(gap, live):
    return jnp.where(iota((SLOTS, 256), 0) < live, jnp.maximum(-gap, 0.0), 0.0)


def total2(x):
    return jnp.sum(jnp.sum(x, axis=0, keepdims=True), axis=1, keepdims=True)


def residual_of(near, pline):
    shape = (SLOTS, SLOTS)
    row = jnp.broadcast_to(pline.astype(F32), shape)
    col = column(pline.astype(F32), 0, SLOTS)
    again = jnp.where((row == col) & (iota(shape, 1) < iota(shape, 0)), 1.0, 0.0)
    first = jnp.sum(again, axis=1, keepdims=True) == 0.0
    square = near[0] * near[0] + near[1] * near[1] + near[2] * near[2]
    return total2(jnp.where(first, square, 0.0))


def respond(normal, energy, node, far, geom, pline, sel, requests, place, out, edge, change):
    lines = [pick(sel[...], normal[c]) for c in range(3)]
    residual = residual_of([v[0:SLOTS] for v in lines], pline)
    tile = pair_tile(energy, residual)
    tile = jnp.concatenate([tile, tile], axis=1)
    for j in range(16):
        out[j, 0:OUTER, :] = jnp.zeros((OUTER, 256), F32)
        out[j, OUTER:24, :] = tile
    x, y = place[0], place[1]
    me = x * 4 + y
    for d, (buf, to, there) in enumerate(
        (
            (requests[0], me - 4, x > 0),
            (requests[1], me + 4, x < 3),
            (requests[2], me - 1, y > 0),
            (requests[3], me + 1, y < 3),
        )
    ):
        at = 2 * SLOTS + OUTER * d
        index = buf[192:208, :].astype(I32)
        answer = jnp.zeros((OUTER, 256), F32)
        for c in range(3):
            value = take_lanes(lines[c][at : at + OUTER], index)
            answer = answer + buf[144 + 16 * c : 160 + 16 * c, :] * value

        @pl.when(there)
        def _():
            out[jnp.where(there, to, 0), 0:OUTER, :] = answer

    z = far[...] - 3
    inside = (z >= 0) & (z < 256)
    index = jnp.clip(z, 0, 255)
    moved = jnp.zeros((SLOTS, 256), F32)
    for c in range(3):
        near = take_lanes(lines[c][0:SLOTS], node[...])
        other = jnp.where(inside, take_lanes(lines[c][SLOTS : 2 * SLOTS], index), 0.0)
        moved = moved + geom[c] * (near - other)
    change[...] = moved
    edge[...] = edge_lanes(normal, 0, 9)


def first_kernel(
    place,
    pos,
    node,
    far,
    geom,
    pline,
    fline,
    live,
    xlo,
    xhi,
    ylo,
    yhi,
    zlo,
    zhi,
    out,
    edge,
    change,
    gap_out,
    normal_out,
    sel_out,
    selz_out,
    inverse_out,
    xs,
    ys,
):
    own = pline[...].astype(F32)
    near_col = column(own, 0, SLOTS)
    far_col = column(fline[...].astype(F32), 0, SLOTS)
    x, y, line = decode(far_col.astype(I32))
    inside = (x >= 0) & (x < 16) & (y >= 0) & (y < 16)
    local = jnp.where(inside, line, -2).astype(F32)
    xo, yo = x[OUTER:], y[OUTER:]
    face = jnp.where(xo < 0, (xo + 3) * 16 + yo, -1)
    face = jnp.where(xo > 15, 48 + (xo - 16) * 16 + yo, face)
    face = jnp.where(yo < 0, 96 + xo * 3 + yo + 3, face)
    face = jnp.where(yo > 15, 144 + xo * 3 + yo - 16, face)
    requests = (xlo, xhi, ylo, yhi)
    wanted = jnp.concatenate(
        [near_col, local] + [buf[208:224, 0:1] - 1.0 for buf in requests], axis=0
    )
    sel = hot(jnp.broadcast_to(own, (128, SLOTS)), wanted)
    sel_out[...] = sel
    selz = jnp.concatenate([zhi[256:257, 0:SLOTS], zlo[256:257, 0:SLOTS]], axis=1) - 1.0
    selz_out[...] = hot(jnp.broadcast_to(selz, (OUTER, 2 * SLOTS)), local[OUTER:])
    lines_f = iota((2 * SLOTS, 256), 1).astype(F32)
    sel_pos = hot(lines_f, jnp.concatenate([near_col, local], axis=0))
    sel_face = hot(iota((OUTER, 192), 1), face)
    lane = iota((256, 128), 1)
    edges = jnp.where(lane < 9, zhi[0:256, :], zlo[0:256, :])
    edges = pick(sel_pos[SLOTS + OUTER :], edges)
    ends = z_values(edges, far[OUTER:, :])
    z = far[...] - 3
    within = (z >= 0) & (z < 256)
    index = jnp.clip(z, 0, 255)
    gap = -geom[3]
    terms = jnp.zeros((SLOTS, 256), F32)
    for c in range(3):
        got = pick(sel_pos, pos[c])
        faces = jnp.concatenate([buf[48 * c : 48 * c + 48, :] for buf in requests], axis=0)
        outer = got[SLOTS + OUTER :] + pick(sel_face, faces)
        near = take_lanes(got[0:SLOTS], node[...])
        other = jnp.concatenate([got[SLOTS : SLOTS + OUTER], outer], axis=0)
        other = jnp.where(within, take_lanes(other, index), 0.0)
        other = other + jnp.concatenate([jnp.zeros((OUTER, 256), F32), ends[c]], axis=0)
        terms = terms + geom[c] * (near - other)
    gap = terms + gap
    gap_out[...] = gap
    depth = depth_of(gap, live[...])
    ones = jnp.where(iota((SLOTS, 256), 0) < live[...], 1.0, 0.0)
    got = scatter([depth * geom[c] for c in range(3)] + [ones], node[...], xs, ys)
    inverse = 1.0 / (1.0 + pick(sel[0:SLOTS], got[3]))
    inverse_out[...] = inverse
    normal = [got[c] * inverse for c in range(3)]
    for c in range(3):
        normal_out[c] = normal[c]
    respond(
        normal, total2(depth * depth), node, far, geom, pline[...], sel_out, requests, place,
        out, edge, change,
    )


def forward_kernel(got, edge, out):
    sums = jnp.sum(got[...], axis=0)[:, :128]
    for j in range(8):
        out[j, 0:SLOTS, :] = edge[...]
        out[j, SLOTS:40, :] = sums


def update(place, gap, change, far, geom, got, gotz, selz):
    sums = jnp.sum(gotz[:, SLOTS:40, :], axis=0)
    energy = sums[0:1, 0:1]
    scale = RELAX * (1.0 / (1.0 + energy / N_PAIRS))
    x, y, k = place[0], place[1], place[2]
    me = x * 4 + y
    outer = jnp.zeros((OUTER, 256), F32)
    for to, there in ((me - 4, x > 0), (me + 4, x < 3), (me - 1, y > 0), (me + 1, y < 3)):
        reply = got[jnp.where(there, to, me), 0:OUTER, :]
        outer = outer + jnp.where(there, reply, 0.0)
    lane = iota((SLOTS, 128), 1)
    above = jnp.where((lane < 9) & (k < 7), gotz[jnp.minimum(k + 1, 7), 0:SLOTS, :], 0.0)
    below = jnp.where((lane >= 9) & (k > 0), gotz[jnp.maximum(k - 1, 0), 0:SLOTS, :], 0.0)
    ends = z_values(
        pick(selz[...], jnp.concatenate([above, below], axis=0)), far[OUTER:, :]
    )
    for c in range(3):
        outer = outer + geom[c, OUTER:, :] * ends[c]
    full = change[...] - jnp.concatenate([jnp.zeros((OUTER, 256), F32), outer], axis=0)
    return sums, scale, gap[...] + scale * full


def sweep_kernel(
    last, place, gap, change, normal, moved, inverse, node, far, geom, pline, live, sel, selz,
    got, gotz, *rest,
):
    if last:
        out, sums_out, normal_out, moved_out, xs, ys = rest
    else:
        xlo, xhi, ylo, yhi = rest[:4]
        out, edge, change_out, gap_out, sums_out, normal_out, moved_out, xs, ys = rest[4:]
    sums, scale, fresh = update(place, gap, change, far, geom, got, gotz, selz)
    sums_out[...] = sums
    for c in range(3):
        moved_out[c] = moved[c] + scale * normal[c]
    depth = depth_of(fresh, live[...])
    energy = total2(depth * depth)
    found = scatter([depth * geom[c] for c in range(3)], node[...], xs, ys)
    fresh_normal = [found[c] * inverse[...] for c in range(3)]
    for c in range(3):
        normal_out[c] = fresh_normal[c]
    if last:
        lines = [pick(sel[0:SLOTS, :], fresh_normal[c]) for c in range(3)]
        tile = pair_tile(energy, residual_of(lines, pline[...]))
        out[...] = jnp.broadcast_to(tile[0:1, :], (128, 128))
    else:
        gap_out[...] = fresh
        respond(
            fresh_normal, energy, node, far, geom, pline[...], sel, (xlo, xhi, ylo, yhi), place,
            out, edge, change_out,
        )


def last_kernel(pos, normal, moved, pline, got, s0, s1, s2, s3, out, history):
    sums = jnp.sum(got[...], axis=0, keepdims=True)
    every = [s[0:1, :] for s in (s0, s1, s2, s3)] + [sums]
    scales = [RELAX * (1.0 / (1.0 + s[:, 0:1] / N_PAIRS)) for s in every]
    sel = hot(iota((256, SLOTS), 0), jnp.broadcast_to(pline[...], (256, SLOTS)))
    for c in range(3):
        out[c] = pos[c] + pick(sel, moved[c] + scales[-1] * normal[c])
    for t in range(SWEEPS):
        residual = scales[t] * scales[t] * every[t][:, 1:2]
        history[0:1, t : t + 1] = jnp.sqrt(1.0 + every[t][:, 0:1] / PAIRS_SLOTS)
        history[1:2, t : t + 1] = jnp.sqrt(1.0 + residual / NODES_BLK)


def call(kernel, outs, args, scratch=(), smem=False, specs=None):
    vmem = pl.BlockSpec(memory_space=pltpu.VMEM)
    in_specs = specs or [vmem] * len(args)
    if smem:
        in_specs = [pl.BlockSpec(memory_space=pltpu.SMEM)] + in_specs[1:]
    return pl.pallas_call(
        kernel,
        out_shape=outs,
        in_specs=in_specs,
        out_specs=jax.tree.map(lambda _: vmem, outs),
        scratch_shapes=list(scratch),
    )(*args)


def shape(*dims, dtype=F32):
    return jax.ShapeDtypeStruct(dims, dtype)


def shift(x, axis, up):
    count = lax.axis_size(axis)
    pairs = [(i, i + 1) for i in range(count - 1)]
    return lax.ppermute(x, axis, pairs if up else [(b, a) for a, b in pairs])


def local(positions, pair_node, pair_line, pair_far, far_line, pair_geom, live_blocks):
    pos = positions.reshape(3, 256, 256)
    node = pair_node.reshape(SLOTS, 256)
    far = pair_far.reshape(SLOTS, 256)
    geom = pair_geom.reshape(SLOTS, 4, 256)
    pline = pair_line.reshape(1, SLOTS)
    fline = far_line.reshape(1, SLOTS)
    live = live_blocks.reshape(1, 1)
    place = jnp.stack([lax.axis_index("gx"), lax.axis_index("gy"), lax.axis_index(GZ)])
    place = place.astype(I32)
    work = [pltpu.VMEM((2, 256, 128), F32)] * 2

    face, ends = shape(224, 256), shape(264, 128)
    xdn, xup, ydn, yup, zdn, zup, geom = call(
        pack_kernel,
        [face] * 4 + [ends] * 2 + [shape(4, SLOTS, 256)],
        [pos, far, geom, fline, pline],
    )
    requests = [
        shift(xup, "gx", True),
        shift(xdn, "gx", False),
        shift(yup, "gy", True),
        shift(ydn, "gy", False),
    ]
    zlo = shift(zup, GZ, True)
    zhi = shift(zdn, GZ, False)
    triple, flat = shape(3, SLOTS, 256), shape(SLOTS, 256)
    outbound, edges = shape(16, 24, 256), shape(SLOTS, 128)
    out, edge, change, gap, normal, sel, selz, inverse = call(
        first_kernel,
        [
            outbound,
            edges,
            flat,
            flat,
            triple,
            shape(128, SLOTS, dtype=BF16),
            shape(OUTER, 2 * SLOTS, dtype=BF16),
            flat,
        ],
        [place, pos, node, far, geom, pline, fline, live, *requests, zlo, zhi],
        work,
        smem=True,
    )
    moved = jnp.zeros((3, SLOTS, 256), F32)
    totals = []
    vmem = pl.BlockSpec(memory_space=pltpu.VMEM)
    for t in range(1, SWEEPS):
        got = lax.all_to_all(out, XY, 0, 0, tiled=True)
        out = pl.pallas_call(
            forward_kernel,
            out_shape=shape(8, 40, 128),
            grid=(1,),
            in_specs=[
                pl.BlockSpec((16, 8, 256), lambda i: (0, 2, 0)),
                pl.BlockSpec((SLOTS, 128), lambda i: (0, 0)),
            ],
            out_specs=pl.BlockSpec((8, 40, 128), lambda i: (0, 0, 0)),
        )(got, edge)
        gotz = lax.all_to_all(out, GZ, 0, 0, tiled=True)
        last = t + 1 == SWEEPS
        args = [
            place, gap, change, normal, moved, inverse, node, far, geom, pline, live, sel, selz,
            got, gotz,
        ]
        sums_shape = shape(8, 128)
        if last:
            out, sums, normal, moved = call(
                functools.partial(sweep_kernel, True),
                [shape(128, 128), sums_shape, triple, triple],
                args,
                work,
                smem=True,
            )
        else:
            out, edge, change, gap, sums, normal, moved = call(
                functools.partial(sweep_kernel, False),
                [outbound, edges, flat, flat, sums_shape, triple, triple],
                args + requests,
                work,
                smem=True,
            )
        totals.append(sums)
    got = lax.all_to_all(out, ALL, 0, 0, tiled=True)
    corrected, history = call(
        last_kernel,
        [shape(3, 256, 256), shape(2, SWEEPS)],
        [pos, normal, moved, pline, got, *totals],
    )
    return corrected.reshape(positions.shape), history


def solution(mesh):
    finer = Mesh(
        mesh.devices.reshape(mesh.shape["gx"], mesh.shape["gy"], 4, 2), ("gx", "gy", "gz_0", "gz_1")
    )
    placed = (
        P(None, "gx", "gy", GZ),
        P("gx", "gy", GZ, None, None),
        P("gx", "gy", GZ, None),
        P("gx", "gy", GZ, None, None),
        P("gx", "gy", GZ, None),
        P("gx", "gy", GZ, None, None, None),
        P("gx", "gy", GZ),
    )
    return jax.shard_map(
        local,
        mesh=finer,
        in_specs=placed,
        out_specs=(P(None, "gx", "gy", GZ), P()),
        check_vma=False,
    )
```

time: 496 us -> 182 us (0.37); the launches traced: 487 us -> 180 us
  matrix products: 104 us -> 0 us
  blocking collectives: 197 us -> 119 us
  starting transfers between devices: 86.6 us -> 15.8 us
  local copies, waits for them, and re-layouts: 48.9 us -> 1.34 us
  Pallas kernels: 0 us -> 37.9 us
  other arithmetic: 35.3 us -> 0.58 us
  between operations: 12.6 us -> 1.42 us
    psum x24 -> x0, blocking collectives: 197 us -> none  [one_axis_at_a_time(): x = lax.psum(x, axis)]
    all_to_all x0 -> x9, blocking collectives: none -> 119 us  [the longest x4 58.4 us: local(): got = lax.all_to_all(out, XY, 0, 0, tiled=True)]
    dot_general x59 -> x0, matrix products: 104 us -> none  [the longest x15 27.1 us: select_lines(): return jnp.einsum('bl,cln->bcn', line_hot, field_lines, precision=highest)]
    ppermute x30 -> x6, starting transfers between devices: 86.6 us -> 15.8 us  [shift(): return lax.ppermute(x, axis, pairs if up else [(b, a) for a, b in pairs])]
    pallas_call x0 -> x11, Pallas kernels: none -> 37.9 us  [the longest x7 31.6 us: call(): pl.pallas_call(kernel, out_shape=outs, in_specs=in_specs, out_specs=jax.t...]
    reshape x10 -> x0, local copies, waits for them, and re-layouts: 26 us -> none  [the longest x5 15.1 us: local(): local_pad = jnp.pad(current, widths).reshape(3, ext_lines, ext_z)]
    concatenate x6 -> x0, other arithmetic: 22.2 us -> none  [the longest x4 18.4 us: with_halo(): jnp.concatenate([jnp.pad(low, around), x, jnp.pad(high, around)], axis=dim)]
    reduce_sum x10 -> x0, other arithmetic: 7.53 us -> none  [sweep_add_group(): return (running, energy_sum + jnp.sum(depth_value * depth_value))]
  transfers between devices with their start and end apart: 30 -> 6, of which waited for: 5 -> 2; matrix products, arithmetic and copies ran while one was open for 10% -> 0% of each run, Pallas kernels for 0% -> 0%
where the time goes in v1:
time: 182 us; the launch traced here: 180 us
  blocking collectives  119 us (65%)
  Pallas kernels  37.9 us (21%)
  starting transfers between devices  15.8 us (9%)
  waiting for transfers between devices  4.73 us (3%)
    all_to_all x4, blocking collectives, local(): got = lax.all_to_all(out, XY, 0, 0, tiled=True)  58.4 us
    all_to_all x4, blocking collectives, local(): gotz = lax.all_to_all(out, GZ, 0, 0, tiled=True)  45 us
    pallas_call x7, Pallas kernels, call(): pl.pallas_call(kernel, out_shape=outs, in_specs=in_specs, out_specs=jax.t...  31.6 us
    ppermute x6, starting transfers between devices, shift(): return lax.ppermute(x, axis, pairs if up else [(b, a) for a, b in pairs])  15.8 us
    all_to_all x1, blocking collectives, local(): got = lax.all_to_all(out, ALL, 0, 0, tiled=True)  15.1 us
    pallas_call x4, Pallas kernels, local(): pl.pallas_call(forward_kernel, out_shape=shape(8, 40, 128), grid=(1,), in...  6.37 us
    ppermute x6, waiting for transfers between devices, shift(): return lax.ppermute(x, axis, pairs if up else [(b, a) for a, b in pairs])  4.73 us
  transfers between devices with their start and end apart: 6, of which 2 were waited for; matrix products, arithmetic and copies ran while one was open for 0% of the time, Pallas kernels for 0%

profile of v1, /device:TPU:1, one launch (start us, length us, event | category | flops | bytes accessed | tf_op | source)
XLA Modules:
  0.0 180.3 jit_solution(2526346242766070901)
XLA Ops:
  0.6 2.4 %shard_map.86 = (f32[224,256]{1,0:T(8,128)}, f32[224,256]{1,0:T(8,128)}, f32[224,256]{1,0:T(8,128)}, f32[224,256]{1,0:T(8,128)}, f32[264,128]{1,0:T(8,128)}, /*index=5*/f32[264,128]{1,0:T(8,128)}, f32[4,32,256]{2,1,0:T(8,128)}) custom-call(f32[3,256,256]{2,1,0:T(8,128)} %bitcast.20, s32[32,256]{1,0:T(8,128)} %bitcast.23, f32[32,4,256]{2,1,0:T(4,128)} %bitcast.35, ...), custom_call_target="tpu_custom_call" | custom-call | tf_op jit(solution)/shard_map/pallas_call | solution.py:400
  3.1 4.5 %collective-permute-start.4 = (f32[264,128]{1,0:T(8,128)}, f32[264,128]{1,0:T(8,128)S(1)}, u32[]{:S(2)}, u32[]{:S(2)}) collective-permute-start(f32[264,128]{1,0:T(8,128)} %get-tuple-element.49), channel_id=1, source_target_pairs={{0,1},{1,2},{2,3},{3,4},{4,5},{5,6},{6,7},{8,9},{9,10},{10,11},{11... | collective-permute-start | bytes 405512 | tf_op jit(solution)/shard_map/ppermute | solution.py:416
  7.6 3.6 %collective-permute-start = (f32[224,256]{1,0:T(8,128)}, f32[224,256]{1,0:T(8,128)S(1)}, u32[]{:S(2)}, u32[]{:S(2)}) collective-permute-start(f32[224,256]{1,0:T(8,128)} %get-tuple-element.45), channel_id=1, source_target_pairs={{0,32},{32,64},{64,96},{1,33},{33,65},{65,97},{2,34},{34,66},{66,9... | collective-permute-start | bytes 688136 | tf_op jit(solution)/shard_map/ppermute | solution.py:416
  11.1 1.3 collective-permute-start.1
  12.4 3.2 %collective-permute-start.2 = (f32[224,256]{1,0:T(8,128)}, f32[224,256]{1,0:T(8,128)S(1)}, u32[]{:S(2)}, u32[]{:S(2)}) collective-permute-start(f32[224,256]{1,0:T(8,128)} %get-tuple-element.47), channel_id=1, source_target_pairs={{0,8},{8,16},{16,24},{1,9},{9,17},{17,25},{2,10},{10,18},{18,26},{... | collective-permute-start | bytes 688136 | tf_op jit(solution)/shard_map/ppermute | solution.py:416
  15.6 1.3 collective-permute-start.3
  16.9 0.0 collective-permute-done.4.zlo
  17.0 0.0 copy-start.4
  17.0 1.9 %collective-permute-start.5 = (f32[264,128]{1,0:T(8,128)}, f32[264,128]{1,0:T(8,128)S(1)}, u32[]{:S(2)}, u32[]{:S(2)}) collective-permute-start(f32[264,128]{1,0:T(8,128)} %get-tuple-element.50), channel_id=1, source_target_pairs={{1,0},{2,1},{3,2},{4,3},{5,4},{6,5},{7,6},{9,8},{10,9},{11,10},{12... | collective-permute-start | bytes 405512 | tf_op jit(solution)/shard_map/ppermute | solution.py:416
  19.6 0.6 pad_add_fusion.place
  20.1 3.7 %collective-permute-done.5.zhi = f32[264,128]{1,0:T(8,128)S(1)} collective-permute-done((f32[264,128]{1,0:T(8,128)}, f32[264,128]{1,0:T(8,128)S(1)}, u32[]{:S(2)}, u32[]{:S(2)}) %collective-permute-start.5) | collective-permute-done | bytes 135200 | tf_op jit(solution)/shard_map/ppermute | solution.py:416
  23.8 0.0 copy-start.5
  23.8 0.0 collective-permute-done.xlo.rest_0_
  23.8 0.0 copy-start
  23.8 0.0 collective-permute-done.1.xhi.rest_1_
  23.8 0.0 copy-start.1
  23.8 0.0 collective-permute-done.2.ylo.rest_2_
  23.8 0.0 copy-start.2
  23.8 1.0 collective-permute-done.3.yhi.rest_3_
  24.9 0.0 copy-start.3
  24.9 0.0 copy-done.4
  24.9 0.0 copy-done.5
  24.9 0.0 copy-done
  24.9 0.0 copy-done.1
  24.9 0.0 copy-done.2
  24.9 0.7 copy-done.3
  25.6 6.1 %shard_map.87 = (f32[16,24,256]{2,1,0:T(8,128)}, f32[32,128]{1,0:T(8,128)}, f32[32,256]{1,0:T(8,128)}, f32[32,256]{1,0:T(8,128)}, f32[3,32,256]{2,1,0:T(8,128)},...) custom-call(s32[3]{0:T(128)} %pad_add_fusion.place, f32[3,256,256]{2,1,0:T(8,128)} %bitcast.21, ...), custom_call_target="tpu_custom_call" | custom-call | tf_op jit(solution)/shard_map/pallas_call | solution.py:400
  31.7 17.9 %all_to_all.51.got = f32[16,24,256]{2,1,0:T(8,128)} all-to-all(f32[16,24,256]{2,1,0:T(8,128)} %get-tuple-element.57), channel_id=1, replica_groups=mesh['gx'=4,'gy'=4,'gz_0'=4,'gz_1'=2] {'gx','gy'}, dimensions={0} | all-to-all | bytes 786432 | tf_op jit(solution)/shard_map/all_to_all | solution.py:467
  49.7 1.6 shard_map.88
  51.2 11.1 %all_to_all.52.gotz = f32[8,40,128]{2,1,0:T(8,128)} all-to-all(f32[8,40,128]{2,1,0:T(8,128)} %shard_map.88), channel_id=1, replica_groups=mesh['gx'=4,'gy'=4,'gz_0'=4,'gz_1'=2] {'gz_0','gz_1'}, dimensions={0} | all-to-all | bytes 327680 | tf_op jit(solution)/shard_map/all_to_all | solution.py:478
  62.3 0.6 broadcast_in_dim.3.moved
  63.0 5.4 %shard_map.89 = (f32[16,24,256]{2,1,0:T(8,128)}, f32[32,128]{1,0:T(8,128)}, f32[32,256]{1,0:T(8,128)}, f32[32,256]{1,0:T(8,128)}, f32[8,128]{1,0:T(8,128)}, /*in...) custom-call(s32[3]{0:T(128)} %pad_add_fusion.place, f32[32,256]{1,0:T(8,128)} %get-tuple-element.51.gap, ...), custom_call_target="tpu_custom_call" | custom-call | tf_op jit(solution)/shard_map/pallas_call | solution.py:400
  68.4 13.5 %all_to_all.53.got = f32[16,24,256]{2,1,0:T(8,128)} all-to-all(f32[16,24,256]{2,1,0:T(8,128)} %get-tuple-element.63), channel_id=1, replica_groups=mesh['gx'=4,'gy'=4,'gz_0'=4,'gz_1'=2] {'gx','gy'}, dimensions={0} | all-to-all | bytes 786432 | tf_op jit(solution)/shard_map/all_to_all | solution.py:467
  81.9 1.6 shard_map.90
  83.5 11.3 %all_to_all.54.gotz = f32[8,40,128]{2,1,0:T(8,128)} all-to-all(f32[8,40,128]{2,1,0:T(8,128)} %shard_map.90), channel_id=1, replica_groups=mesh['gx'=4,'gy'=4,'gz_0'=4,'gz_1'=2] {'gz_0','gz_1'}, dimensions={0} | all-to-all | bytes 327680 | tf_op jit(solution)/shard_map/all_to_all | solution.py:478
  94.8 5.4 %shard_map.91 = (f32[16,24,256]{2,1,0:T(8,128)}, f32[32,128]{1,0:T(8,128)}, f32[32,256]{1,0:T(8,128)}, f32[32,256]{1,0:T(8,128)}, f32[8,128]{1,0:T(8,128)}, /*in...) custom-call(s32[3]{0:T(128)} %pad_add_fusion.place, f32[32,256]{1,0:T(8,128)} %get-tuple-element.59.gap, ...), custom_call_target="tpu_custom_call" | custom-call | tf_op jit(solution)/shard_map/pallas_call | solution.py:400
  100.2 13.5 %all_to_all.55.got = f32[16,24,256]{2,1,0:T(8,128)} all-to-all(f32[16,24,256]{2,1,0:T(8,128)} %get-tuple-element.69), channel_id=1, replica_groups=mesh['gx'=4,'gy'=4,'gz_0'=4,'gz_1'=2] {'gx','gy'}, dimensions={0} | all-to-all | bytes 786432 | tf_op jit(solution)/shard_map/all_to_all | solution.py:467
  113.7 1.6 shard_map.92
  115.3 11.3 %all_to_all.56.gotz = f32[8,40,128]{2,1,0:T(8,128)} all-to-all(f32[8,40,128]{2,1,0:T(8,128)} %shard_map.92), channel_id=1, replica_groups=mesh['gx'=4,'gy'=4,'gz_0'=4,'gz_1'=2] {'gz_0','gz_1'}, dimensions={0} | all-to-all | bytes 327680 | tf_op jit(solution)/shard_map/all_to_all | solution.py:478
  126.6 5.4 %shard_map.93 = (f32[16,24,256]{2,1,0:T(8,128)}, f32[32,128]{1,0:T(8,128)}, f32[32,256]{1,0:T(8,128)}, f32[32,256]{1,0:T(8,128)}, f32[8,128]{1,0:T(8,128)}, /*in...) custom-call(s32[3]{0:T(128)} %pad_add_fusion.place, f32[32,256]{1,0:T(8,128)} %get-tuple-element.65.gap, ...), custom_call_target="tpu_custom_call" | custom-call | tf_op jit(solution)/shard_map/pallas_call | solution.py:400
  131.9 13.5 %all_to_all.57.got = f32[16,24,256]{2,1,0:T(8,128)} all-to-all(f32[16,24,256]{2,1,0:T(8,128)} %get-tuple-element.75), channel_id=1, replica_groups=mesh['gx'=4,'gy'=4,'gz_0'=4,'gz_1'=2] {'gx','gy'}, dimensions={0} | all-to-all | bytes 786432 | tf_op jit(solution)/shard_map/all_to_all | solution.py:467
  145.4 1.6 shard_map.94
  147.0 11.3 %all_to_all.58.gotz = f32[8,40,128]{2,1,0:T(8,128)} all-to-all(f32[8,40,128]{2,1,0:T(8,128)} %shard_map.94), channel_id=1, replica_groups=mesh['gx'=4,'gy'=4,'gz_0'=4,'gz_1'=2] {'gz_0','gz_1'}, dimensions={0} | all-to-all | bytes 327680 | tf_op jit(solution)/shard_map/all_to_all | solution.py:478
  158.3 4.2 %shard_map.95 = (f32[128,128]{1,0:T(8,128)}, f32[8,128]{1,0:T(8,128)}, f32[3,32,256]{2,1,0:T(8,128)}, f32[3,32,256]{2,1,0:T(8,128)}) custom-call(s32[3]{0:T(128)} %pad_add_fusion.place, f32[32,256]{1,0:T(8,128)} %get-tuple-element.71.gap, f32[32,256]{1,0:T(8,128)} %get-tuple-element.72.change, f32[3,32,256]{2,1,0:T(8,128)} %get-tuple-element.73.normal, ...), custom_call_target="tpu_custom_call" | custom-call | tf_op jit(solution)/shard_map/pallas_call | solution.py:400
  162.6 15.1 %all_to_all.59 = f32[128,1,128]{2,1,0:T(1,128)} all-to-all(f32[128,1,128]{2,1,0:T(1,128)} %bitcast.36), channel_id=1, replica_groups=mesh['gx'=4,'gy'=4,'gz_0'=4,'gz_1'=2] {'gx','gy','gz_0','gz_1'}, dimensions={0} | all-to-all | bytes 131072 | tf_op jit(solution)/shard_map/all_to_all | solution.py:502
  177.6 2.7 %shard_map.96 = (f32[3,256,256]{2,1,0:T(8,128)}, f32[2,5]{1,0:T(2,128)}) custom-call(f32[3,256,256]{2,1,0:T(8,128)} %bitcast.22, f32[3,32,256]{2,1,0:T(8,128)} %get-tuple-element.77.normal, f32[3,32,256]{2,1,0:T(8,128)} %get-tuple-element.78.moved, s32[1,32]{1,0:T(1,128)} %bitcast.43, f32[128,128]{1,0:T(8,128)} %bitcast.34, f32[8,128]{1,0:T(8,128)} %get-tuple-element.80.s0, ...), custom_call_target="tpu_custom_call" | custom-call | tf_op jit(solution)/shard_map/pallas_call | solution.py:400
Async XLA Ops:
  3.1 13.9 %collective-permute-start.4 = (f32[264,128]{1,0:T(8,128)}, f32[264,128]{1,0:T(8,128)S(1)}, u32[]{:S(2)}, u32[]{:S(2)}) collective-permute-start(f32[264,128]{1,0:T(8,128)} %get-tuple-element.49), channel_id=1, source_target_pairs={{0,1},{1,2},{2,3},{3,4},{4,5},{5,6},{6,7},{8,9},{9,10},{10,11},{11... | collective-permute-start | bytes 405512 | tf_op jit(solution)/shard_map/ppermute | solution.py:416
  7.6 16.2 %collective-permute-start = (f32[224,256]{1,0:T(8,128)}, f32[224,256]{1,0:T(8,128)S(1)}, u32[]{:S(2)}, u32[]{:S(2)}) collective-permute-start(f32[224,256]{1,0:T(8,128)} %get-tuple-element.45), channel_id=1, source_target_pairs={{0,32},{32,64},{64,96},{1,33},{33,65},{65,97},{2,34},{34,66},{66,9... | collective-permute-start | bytes 688136 | tf_op jit(solution)/shard_map/ppermute | solution.py:416
  11.1 12.7 %collective-permute-start.1 = (f32[224,256]{1,0:T(8,128)}, f32[224,256]{1,0:T(8,128)S(1)}, u32[]{:S(2)}, u32[]{:S(2)}) collective-permute-start(f32[224,256]{1,0:T(8,128)} %get-tuple-element.46), channel_id=1, source_target_pairs={{32,0},{64,32},{96,64},{33,1},{65,33},{97,65},{34,2},{66,34},{98,6... | collective-permute-start | bytes 688136 | tf_op jit(solution)/shard_map/ppermute | solution.py:416
  12.4 11.4 %collective-permute-start.2 = (f32[224,256]{1,0:T(8,128)}, f32[224,256]{1,0:T(8,128)S(1)}, u32[]{:S(2)}, u32[]{:S(2)}) collective-permute-start(f32[224,256]{1,0:T(8,128)} %get-tuple-element.47), channel_id=1, source_target_pairs={{0,8},{8,16},{16,24},{1,9},{9,17},{17,25},{2,10},{10,18},{18,26},{... | collective-permute-start | bytes 688136 | tf_op jit(solution)/shard_map/ppermute | solution.py:416
  15.6 9.2 %collective-permute-start.3 = (f32[224,256]{1,0:T(8,128)}, f32[224,256]{1,0:T(8,128)S(1)}, u32[]{:S(2)}, u32[]{:S(2)}) collective-permute-start(f32[224,256]{1,0:T(8,128)} %get-tuple-element.48), channel_id=1, source_target_pairs={{8,0},{16,8},{24,16},{9,1},{17,9},{25,17},{10,2},{18,10},{26,18},{... | collective-permute-start | bytes 688136 | tf_op jit(solution)/shard_map/ppermute | solution.py:416
  17.0 7.9 %copy-start.4 = (f32[264,128]{1,0:T(8,128)}, f32[264,128]{1,0:T(8,128)S(1)}, u32[]{:S(2)}) copy-start(f32[264,128]{1,0:T(8,128)S(1)} %collective-permute-done.4.zlo) | copy-start | bytes 405508
  17.0 6.8 %collective-permute-start.5 = (f32[264,128]{1,0:T(8,128)}, f32[264,128]{1,0:T(8,128)S(1)}, u32[]{:S(2)}, u32[]{:S(2)}) collective-permute-start(f32[264,128]{1,0:T(8,128)} %get-tuple-element.50), channel_id=1, source_target_pairs={{1,0},{2,1},{3,2},{4,3},{5,4},{6,5},{7,6},{9,8},{10,9},{11,10},{12... | collective-permute-start | bytes 405512 | tf_op jit(solution)/shard_map/ppermute | solution.py:416
  23.8 1.1 copy-start.5
  23.8 1.1 copy-start
  23.8 1.1 copy-start.1
  23.8 1.1 copy-start.2
  24.9 0.7 copy-start.3

commit v2 on v1

--- a/solution.py
+++ b/solution.py
@@ -89,7 +89,11 @@
     return out
 
 
-def pack_kernel(pos, far, geom, fline, pline, xdn, xup, ydn, yup, zdn, zup, geom_out):
+def pack_kernel(
+    pos, node, far, geom, pline, fline, live, xdn, xup, ydn, yup, zdn, zup, geom_out, *copies
+):
+    for source, copy in zip((pos, node, far, pline, fline, live), copies, strict=True):
+        copy[...] = source[...]
     for c in range(4):
         geom_out[c] = geom[:, c, :]
     fcol = column(fline[...].astype(F32), OUTER, OUTER).astype(I32)
@@ -196,7 +200,7 @@
     return total2(jnp.where(first, square, 0.0))
 
 
-def respond(normal, energy, node, far, geom, pline, sel, requests, place, out, edge, change):
+def respond(normal, energy, node, far, geom, pline, sel, requests, out, edge, change):
     lines = [pick(sel[...], normal[c]) for c in range(3)]
     residual = residual_of([v[0:SLOTS] for v in lines], pline)
     tile = pair_tile(energy, residual)
@@ -204,7 +208,7 @@
     for j in range(16):
         out[j, 0:OUTER, :] = jnp.zeros((OUTER, 256), F32)
         out[j, OUTER:24, :] = tile
-    x, y = place[0], place[1]
+    x, y, _ = position()
     me = x * 4 + y
     for d, (buf, to, there) in enumerate(
         (
@@ -238,7 +242,6 @@
 
 
 def first_kernel(
-    place,
     pos,
     node,
     far,
@@ -257,6 +260,7 @@
     change,
     gap_out,
     normal_out,
+    moved_out,
     sel_out,
     selz_out,
     inverse_out,
@@ -313,24 +317,25 @@
     normal = [got[c] * inverse for c in range(3)]
     for c in range(3):
         normal_out[c] = normal[c]
+        moved_out[c] = jnp.zeros((SLOTS, 256), F32)
     respond(
-        normal, total2(depth * depth), node, far, geom, pline[...], sel_out, requests, place,
-        out, edge, change,
+        normal, total2(depth * depth), node, far, geom, pline[...], sel_out, requests, out, edge,
+        change,
     )
 
 
 def forward_kernel(got, edge, out):
-    sums = jnp.sum(got[...], axis=0)[:, :128]
+    sums = jnp.sum(got[:, OUTER:24, 0:128], axis=0)
     for j in range(8):
         out[j, 0:SLOTS, :] = edge[...]
         out[j, SLOTS:40, :] = sums
 
 
-def update(place, gap, change, far, geom, got, gotz, selz):
+def update(gap, change, far, geom, got, gotz, selz):
     sums = jnp.sum(gotz[:, SLOTS:40, :], axis=0)
     energy = sums[0:1, 0:1]
     scale = RELAX * (1.0 / (1.0 + energy / N_PAIRS))
-    x, y, k = place[0], place[1], place[2]
+    x, y, k = position()
     me = x * 4 + y
     outer = jnp.zeros((OUTER, 256), F32)
     for to, there in ((me - 4, x > 0), (me + 4, x < 3), (me - 1, y > 0), (me + 1, y < 3)):
@@ -349,7 +354,7 @@
 
 
 def sweep_kernel(
-    last, place, gap, change, normal, moved, inverse, node, far, geom, pline, live, sel, selz,
+    last, gap, change, normal, moved, inverse, node, far, geom, pline, live, sel, selz,
     got, gotz, *rest,
 ):
     if last:
@@ -357,7 +362,7 @@
     else:
         xlo, xhi, ylo, yhi = rest[:4]
         out, edge, change_out, gap_out, sums_out, normal_out, moved_out, xs, ys = rest[4:]
-    sums, scale, fresh = update(place, gap, change, far, geom, got, gotz, selz)
+    sums, scale, fresh = update(gap, change, far, geom, got, gotz, selz)
     sums_out[...] = sums
     for c in range(3):
         moved_out[c] = moved[c] + scale * normal[c]
@@ -374,8 +379,8 @@
     else:
         gap_out[...] = fresh
         respond(
-            fresh_normal, energy, node, far, geom, pline[...], sel, (xlo, xhi, ylo, yhi), place,
-            out, edge, change_out,
+            fresh_normal, energy, node, far, geom, pline[...], sel, (xlo, xhi, ylo, yhi), out, edge,
+            change_out,
         )
 
 
@@ -392,22 +397,28 @@
         history[1:2, t : t + 1] = jnp.sqrt(1.0 + residual / NODES_BLK)
 
 
-def call(kernel, outs, args, scratch=(), smem=False, specs=None):
+def position():
+    return lax.axis_index("gx"), lax.axis_index("gy"), lax.axis_index(GZ)
+
+
+def call(kernel, outs, args, scratch=(), inputs=False):
     vmem = pl.BlockSpec(memory_space=pltpu.VMEM)
-    in_specs = specs or [vmem] * len(args)
-    if smem:
-        in_specs = [pl.BlockSpec(memory_space=pltpu.SMEM)] + in_specs[1:]
     return pl.pallas_call(
         kernel,
         out_shape=outs,
-        in_specs=in_specs,
-        out_specs=jax.tree.map(lambda _: vmem, outs),
+        in_specs=[vmem] * len(args),
+        out_specs=[vmem] * len(outs) if isinstance(outs, list) else vmem,
         scratch_shapes=list(scratch),
-    )(*args)
+        compiler_params=pltpu.CompilerParams(vmem_limit_bytes=12 * 2**20),
+    )(*(args if inputs else [in_vmem(x) for x in args]))
 
 
 def shape(*dims, dtype=F32):
-    return jax.ShapeDtypeStruct(dims, dtype)
+    return pltpu.VMEM(dims, dtype)
+
+
+def in_vmem(x):
+    return pltpu.with_memory_space_constraint(x, pltpu.VMEM)
 
 
 def shift(x, axis, up):
@@ -424,16 +435,22 @@
     pline = pair_line.reshape(1, SLOTS)
     fline = far_line.reshape(1, SLOTS)
     live = live_blocks.reshape(1, 1)
-    place = jnp.stack([lax.axis_index("gx"), lax.axis_index("gy"), lax.axis_index(GZ)])
-    place = place.astype(I32)
     work = [pltpu.VMEM((2, 256, 128), F32)] * 2
 
     face, ends = shape(224, 256), shape(264, 128)
-    xdn, xup, ydn, yup, zdn, zup, geom = call(
+    flat = shape(SLOTS, 256)
+    flat_i = shape(SLOTS, 256, dtype=I32)
+    few = shape(1, SLOTS, dtype=I32)
+    packed = call(
         pack_kernel,
-        [face] * 4 + [ends] * 2 + [shape(4, SLOTS, 256)],
-        [pos, far, geom, fline, pline],
-    )
+        [face] * 4
+        + [ends] * 2
+        + [shape(4, SLOTS, 256), shape(3, 256, 256), flat_i, flat_i, few, few]
+        + [shape(1, 1, dtype=I32)],
+        [pos, node, far, geom, pline, fline, live],
+        inputs=True,
+    )
+    xdn, xup, ydn, yup, zdn, zup, geom, pos, node, far, pline, fline, live = packed
     requests = [
         shift(xup, "gx", True),
         shift(xdn, "gx", False),
@@ -442,9 +459,9 @@
     ]
     zlo = shift(zup, GZ, True)
     zhi = shift(zdn, GZ, False)
-    triple, flat = shape(3, SLOTS, 256), shape(SLOTS, 256)
+    triple = shape(3, SLOTS, 256)
     outbound, edges = shape(16, 24, 256), shape(SLOTS, 128)
-    out, edge, change, gap, normal, sel, selz, inverse = call(
+    out, edge, change, gap, normal, moved, sel, selz, inverse = call(
         first_kernel,
         [
             outbound,
@@ -452,33 +469,22 @@
             flat,
             flat,
             triple,
+            triple,
             shape(128, SLOTS, dtype=BF16),
             shape(OUTER, 2 * SLOTS, dtype=BF16),
             flat,
         ],
-        [place, pos, node, far, geom, pline, fline, live, *requests, zlo, zhi],
+        [pos, node, far, geom, pline, fline, live, *requests, zlo, zhi],
         work,
-        smem=True,
-    )
-    moved = jnp.zeros((3, SLOTS, 256), F32)
+    )
     totals = []
-    vmem = pl.BlockSpec(memory_space=pltpu.VMEM)
     for t in range(1, SWEEPS):
         got = lax.all_to_all(out, XY, 0, 0, tiled=True)
-        out = pl.pallas_call(
-            forward_kernel,
-            out_shape=shape(8, 40, 128),
-            grid=(1,),
-            in_specs=[
-                pl.BlockSpec((16, 8, 256), lambda i: (0, 2, 0)),
-                pl.BlockSpec((SLOTS, 128), lambda i: (0, 0)),
-            ],
-            out_specs=pl.BlockSpec((8, 40, 128), lambda i: (0, 0, 0)),
-        )(got, edge)
+        out = call(forward_kernel, shape(8, 40, 128), [got, edge])
         gotz = lax.all_to_all(out, GZ, 0, 0, tiled=True)
         last = t + 1 == SWEEPS
         args = [
-            place, gap, change, normal, moved, inverse, node, far, geom, pline, live, sel, selz,
+            gap, change, normal, moved, inverse, node, far, geom, pline, live, sel, selz,
             got, gotz,
         ]
         sums_shape = shape(8, 128)
@@ -488,7 +494,6 @@
                 [shape(128, 128), sums_shape, triple, triple],
                 args,
                 work,
-                smem=True,
             )
         else:
             out, edge, change, gap, sums, normal, moved = call(
@@ -496,13 +501,12 @@
                 [outbound, edges, flat, flat, sums_shape, triple, triple],
                 args + requests,
                 work,
-                smem=True,
             )
         totals.append(sums)
     got = lax.all_to_all(out, ALL, 0, 0, tiled=True)
     corrected, history = call(
         last_kernel,
-        [shape(3, 256, 256), shape(2, SWEEPS)],
+        [jax.ShapeDtypeStruct((3, 256, 256), F32), jax.ShapeDtypeStruct((2, SWEEPS), F32)],
         [pos, normal, moved, pline, got, *totals],
     )
     return corrected.reshape(positions.shape), history

time: 182 us -> 156 us (0.86)
  Pallas kernels: 37.9 us -> 21.3 us
  blocking collectives: 119 us -> 106 us
  local copies, waits for them, and re-layouts: 1.34 us -> 4.21 us
    pallas_call x11, Pallas kernels: 37.9 us -> 21.3 us  [call(): pl.pallas_call(kernel, out_shape=outs, in_specs=[vmem] * len(args), out_s...]
    all_to_all x4, blocking collectives: 58.4 us -> 52.5 us  [local(): got = lax.all_to_all(out, XY, 0, 0, tiled=True)]
    all_to_all x4, blocking collectives: 45 us -> 40.4 us  [local(): gotz = lax.all_to_all(out, GZ, 0, 0, tiled=True)]
    unnamed x12, local copies, waits for them, and re-layouts: 0.69 us -> 4.21 us
where the time goes in v2:
time: 156 us; the launch traced here: 155 us
  blocking collectives  106 us (68%)
  Pallas kernels  21.3 us (14%)
  starting transfers between devices  15.8 us (10%)
  waiting for transfers between devices  5.8 us (4%)
  local copies, waits for them, and re-layouts  4.21 us (3%)
    all_to_all x4, blocking collectives, local(): got = lax.all_to_all(out, XY, 0, 0, tiled=True)  52.5 us
    all_to_all x4, blocking collectives, local(): gotz = lax.all_to_all(out, GZ, 0, 0, tiled=True)  40.4 us
    pallas_call x11, Pallas kernels, call(): pl.pallas_call(kernel, out_shape=outs, in_specs=[vmem] * len(args), out_s...  21.3 us
    ppermute x6, starting transfers between devices, shift(): return lax.ppermute(x, axis, pairs if up else [(b, a) for a, b in pairs])  15.8 us
    all_to_all x1, blocking collectives, local(): got = lax.all_to_all(out, ALL, 0, 0, tiled=True)  13.5 us
    ppermute x6, waiting for transfers between devices, shift(): return lax.ppermute(x, axis, pairs if up else [(b, a) for a, b in pairs])  5.8 us
    unnamed x12, local copies, waits for them, and re-layouts  4.21 us
  transfers between devices with their start and end apart: 6, of which 2 were waited for; matrix products, arithmetic and copies ran while one was open for 0% of the time, Pallas kernels for 0%

profile of v2, /device:TPU:1, one launch (start us, length us, event | category | flops | bytes accessed | tf_op | source)
XLA Modules:
  0.0 154.9 jit_solution(5664235266907065932)
XLA Ops:
  1.3 0.0 copy-start.4
  1.3 0.0 copy-start.5
  1.3 0.6 copy-done.4
  1.9 0.0 copy-done.5
  2.0 0.0 copy-start
  2.0 1.1 copy-done
  3.1 0.0 copy-start.1
  3.1 0.9 copy-done.1
  4.0 0.0 copy-start.2
  4.0 0.8 copy-done.2
  4.7 0.0 copy-start.3
  4.7 0.8 copy-done.3
  5.5 0.8 shard_map.86
  6.3 4.5 %collective-permute-start.4 = (f32[264,128]{1,0:T(8,128)S(1)}, f32[264,128]{1,0:T(8,128)S(1)}, u32[]{:S(2)}, u32[]{:S(2)}) collective-permute-start(f32[264,128]{1,0:T(8,128)S(1)} %get-tuple-element.62), channel_id=1, source_target_pairs={{0,1},{1,2},{2,3},{3,4},{4,5},{5,6},{6,7},{8,9},{9,10},{10,11},{11... | collective-permute-start | bytes 405512 | tf_op jit(solution)/shard_map/ppermute | solution.py:427
  10.8 3.6 %collective-permute-start = (f32[224,256]{1,0:T(8,128)S(1)}, f32[224,256]{1,0:T(8,128)S(1)}, u32[]{:S(2)}, u32[]{:S(2)}) collective-permute-start(f32[224,256]{1,0:T(8,128)S(1)} %get-tuple-element.58), channel_id=1, source_target_pairs={{0,32},{32,64},{64,96},{1,33},{33,65},{65,97},{2,34},{34,66},{66,9... | collective-permute-start | bytes 688136 | tf_op jit(solution)/shard_map/ppermute | solution.py:427
  14.3 1.3 collective-permute-start.1
  15.6 3.2 %collective-permute-start.2 = (f32[224,256]{1,0:T(8,128)S(1)}, f32[224,256]{1,0:T(8,128)S(1)}, u32[]{:S(2)}, u32[]{:S(2)}) collective-permute-start(f32[224,256]{1,0:T(8,128)S(1)} %get-tuple-element.60), channel_id=1, source_target_pairs={{0,8},{8,16},{16,24},{1,9},{9,17},{17,25},{2,10},{10,18},{18,26},{... | collective-permute-start | bytes 688136 | tf_op jit(solution)/shard_map/ppermute | solution.py:427
  18.8 1.3 collective-permute-start.3
  20.1 0.0 collective-permute-done.4.zlo
  20.2 1.9 %collective-permute-start.5 = (f32[264,128]{1,0:T(8,128)S(1)}, f32[264,128]{1,0:T(8,128)S(1)}, u32[]{:S(2)}, u32[]{:S(2)}) collective-permute-start(f32[264,128]{1,0:T(8,128)S(1)} %get-tuple-element.63), channel_id=1, source_target_pairs={{1,0},{2,1},{3,2},{4,3},{5,4},{6,5},{7,6},{9,8},{10,9},{11,10},{12... | collective-permute-start | bytes 405512 | tf_op jit(solution)/shard_map/ppermute | solution.py:427
  22.1 4.7 %collective-permute-done.5.zhi = f32[264,128]{1,0:T(8,128)S(1)} collective-permute-done((f32[264,128]{1,0:T(8,128)S(1)}, f32[264,128]{1,0:T(8,128)S(1)}, u32[]{:S(2)}, u32[]{:S(2)}) %collective-permute-start.5) | collective-permute-done | bytes 135200 | tf_op jit(solution)/shard_map/ppermute | solution.py:427
  26.8 0.0 collective-permute-done.xlo.rest_0_
  26.8 0.0 collective-permute-done.1.xhi.rest_1_
  26.8 0.0 collective-permute-done.2.ylo.rest_2_
  26.8 1.1 collective-permute-done.3.yhi.rest_3_
  27.9 4.5 %shard_map.87 = (f32[16,24,256]{2,1,0:T(8,128)S(1)}, f32[32,128]{1,0:T(8,128)S(1)}, f32[32,256]{1,0:T(8,128)S(1)}, f32[32,256]{1,0:T(8,128)S(1)}, f32[3,32,256]{...) custom-call(f32[3,256,256]{2,1,0:T(8,128)S(1)} %get-tuple-element.51, ...), custom_call_target="tpu_custom_call" | custom-call | tf_op jit(solution)/shard_map/pallas_call | solution.py:406
  32.4 17.6 %all_to_all.51.got = f32[16,24,256]{2,1,0:T(8,128)S(1)} all-to-all(f32[16,24,256]{2,1,0:T(8,128)S(1)} %get-tuple-element.71), channel_id=1, replica_groups=mesh['gx'=4,'gy'=4,'gz_0'=4,'gz_1'=2] {'gx','gy'}, dimensions={0} | all-to-all | bytes 786432 | tf_op jit(solution)/shard_map/all_to_all | solution.py:482
  50.1 10.5 %all_to_all.52.gotz = f32[8,40,128]{2,1,0:T(8,128)S(1)} all-to-all(f32[8,40,128]{2,1,0:T(8,128)S(1)} %shard_map.88), channel_id=1, replica_groups=mesh['gx'=4,'gy'=4,'gz_0'=4,'gz_1'=2] {'gz_0','gz_1'}, dimensions={0} | all-to-all | bytes 327680 | tf_op jit(solution)/shard_map/all_to_all | solution.py:484
  60.5 3.8 %shard_map.89 = (f32[16,24,256]{2,1,0:T(8,128)S(1)}, f32[32,128]{1,0:T(8,128)S(1)}, f32[32,256]{1,0:T(8,128)S(1)}, f32[32,256]{1,0:T(8,128)S(1)}, f32[8,128]{1,0...) custom-call(f32[32,256]{1,0:T(8,128)S(1)} %get-tuple-element.64.gap, ...), custom_call_target="tpu_custom_call" | custom-call | tf_op jit(solution)/shard_map/pallas_call | solution.py:406
  64.4 11.6 %all_to_all.53.got = f32[16,24,256]{2,1,0:T(8,128)S(1)} all-to-all(f32[16,24,256]{2,1,0:T(8,128)S(1)} %get-tuple-element.77), channel_id=1, replica_groups=mesh['gx'=4,'gy'=4,'gz_0'=4,'gz_1'=2] {'gx','gy'}, dimensions={0} | all-to-all | bytes 786432 | tf_op jit(solution)/shard_map/all_to_all | solution.py:482
  76.0 10.0 %all_to_all.54.gotz = f32[8,40,128]{2,1,0:T(8,128)S(1)} all-to-all(f32[8,40,128]{2,1,0:T(8,128)S(1)} %shard_map.90), channel_id=1, replica_groups=mesh['gx'=4,'gy'=4,'gz_0'=4,'gz_1'=2] {'gz_0','gz_1'}, dimensions={0} | all-to-all | bytes 327680 | tf_op jit(solution)/shard_map/all_to_all | solution.py:484
  86.0 3.8 %shard_map.91 = (f32[16,24,256]{2,1,0:T(8,128)S(1)}, f32[32,128]{1,0:T(8,128)S(1)}, f32[32,256]{1,0:T(8,128)S(1)}, f32[32,256]{1,0:T(8,128)S(1)}, f32[8,128]{1,0...) custom-call(f32[32,256]{1,0:T(8,128)S(1)} %get-tuple-element.73.gap, ...), custom_call_target="tpu_custom_call" | custom-call | tf_op jit(solution)/shard_map/pallas_call | solution.py:406
  89.9 11.6 %all_to_all.55.got = f32[16,24,256]{2,1,0:T(8,128)S(1)} all-to-all(f32[16,24,256]{2,1,0:T(8,128)S(1)} %get-tuple-element.83), channel_id=1, replica_groups=mesh['gx'=4,'gy'=4,'gz_0'=4,'gz_1'=2] {'gx','gy'}, dimensions={0} | all-to-all | bytes 786432 | tf_op jit(solution)/shard_map/all_to_all | solution.py:482
  101.5 10.0 %all_to_all.56.gotz = f32[8,40,128]{2,1,0:T(8,128)S(1)} all-to-all(f32[8,40,128]{2,1,0:T(8,128)S(1)} %shard_map.92), channel_id=1, replica_groups=mesh['gx'=4,'gy'=4,'gz_0'=4,'gz_1'=2] {'gz_0','gz_1'}, dimensions={0} | all-to-all | bytes 327680 | tf_op jit(solution)/shard_map/all_to_all | solution.py:484
  111.5 3.8 %shard_map.93 = (f32[16,24,256]{2,1,0:T(8,128)S(1)}, f32[32,128]{1,0:T(8,128)S(1)}, f32[32,256]{1,0:T(8,128)S(1)}, f32[32,256]{1,0:T(8,128)S(1)}, f32[8,128]{1,0...) custom-call(f32[32,256]{1,0:T(8,128)S(1)} %get-tuple-element.79.gap, ...), custom_call_target="tpu_custom_call" | custom-call | tf_op jit(solution)/shard_map/pallas_call | solution.py:406
  115.3 11.6 %all_to_all.57.got = f32[16,24,256]{2,1,0:T(8,128)S(1)} all-to-all(f32[16,24,256]{2,1,0:T(8,128)S(1)} %get-tuple-element.89), channel_id=1, replica_groups=mesh['gx'=4,'gy'=4,'gz_0'=4,'gz_1'=2] {'gx','gy'}, dimensions={0} | all-to-all | bytes 786432 | tf_op jit(solution)/shard_map/all_to_all | solution.py:482
  127.0 10.0 %all_to_all.58.gotz = f32[8,40,128]{2,1,0:T(8,128)S(1)} all-to-all(f32[8,40,128]{2,1,0:T(8,128)S(1)} %shard_map.94), channel_id=1, replica_groups=mesh['gx'=4,'gy'=4,'gz_0'=4,'gz_1'=2] {'gz_0','gz_1'}, dimensions={0} | all-to-all | bytes 327680 | tf_op jit(solution)/shard_map/all_to_all | solution.py:484
  136.9 3.0 %shard_map.95 = (f32[128,128]{1,0:T(8,128)S(1)}, f32[8,128]{1,0:T(8,128)S(1)}, f32[3,32,256]{2,1,0:T(8,128)S(1)}, f32[3,32,256]{2,1,0:T(8,128)S(1)}) custom-call(f32[32,256]{1,0:T(8,128)S(1)} %get-tuple-element.85.gap, f32[32,256]{1,0:T(8,128)S(1)} %get-tuple-element.86.change, f32[3,32,256]{2,1,0:T(8,128)S(1)} %get-tuple-element.87.normal, ...), custom_call_target="tpu_custom_call" | custom-call | tf_op jit(solution)/shard_map/pallas_call | solution.py:406
  139.9 13.5 %all_to_all.59 = f32[128,1,128]{2,1,0:T(1,128)S(1)} all-to-all(f32[128,1,128]{2,1,0:T(1,128)S(1)} %bitcast.16), channel_id=1, replica_groups=mesh['gx'=4,'gy'=4,'gz_0'=4,'gz_1'=2] {'gx','gy','gz_0','gz_1'}, dimensions={0} | all-to-all | bytes 131072 | tf_op jit(solution)/shard_map/all_to_all | solution.py:506
  153.4 1.4 shard_map.96
  (4 shorter events, 0.1 us)
Async XLA Ops:
  1.3 0.7 copy-start.4
  1.3 0.7 copy-start.5
  2.0 1.1 copy-start
  3.1 0.9 copy-start.1
  4.0 0.8 copy-start.2
  4.7 0.8 copy-start.3
  6.3 13.9 %collective-permute-start.4 = (f32[264,128]{1,0:T(8,128)S(1)}, f32[264,128]{1,0:T(8,128)S(1)}, u32[]{:S(2)}, u32[]{:S(2)}) collective-permute-start(f32[264,128]{1,0:T(8,128)S(1)} %get-tuple-element.62), channel_id=1, source_target_pairs={{0,1},{1,2},{2,3},{3,4},{4,5},{5,6},{6,7},{8,9},{9,10},{10,11},{11... | collective-permute-start | bytes 405512 | tf_op jit(solution)/shard_map/ppermute | solution.py:427
  10.8 16.0 %collective-permute-start = (f32[224,256]{1,0:T(8,128)S(1)}, f32[224,256]{1,0:T(8,128)S(1)}, u32[]{:S(2)}, u32[]{:S(2)}) collective-permute-start(f32[224,256]{1,0:T(8,128)S(1)} %get-tuple-element.58), channel_id=1, source_target_pairs={{0,32},{32,64},{64,96},{1,33},{33,65},{65,97},{2,34},{34,66},{66,9... | collective-permute-start | bytes 688136 | tf_op jit(solution)/shard_map/ppermute | solution.py:427
  14.3 12.5 %collective-permute-start.1 = (f32[224,256]{1,0:T(8,128)S(1)}, f32[224,256]{1,0:T(8,128)S(1)}, u32[]{:S(2)}, u32[]{:S(2)}) collective-permute-start(f32[224,256]{1,0:T(8,128)S(1)} %get-tuple-element.59), channel_id=1, source_target_pairs={{32,0},{64,32},{96,64},{33,1},{65,33},{97,65},{34,2},{66,34},{98,6... | collective-permute-start | bytes 688136 | tf_op jit(solution)/shard_map/ppermute | solution.py:427
  15.6 11.2 %collective-permute-start.2 = (f32[224,256]{1,0:T(8,128)S(1)}, f32[224,256]{1,0:T(8,128)S(1)}, u32[]{:S(2)}, u32[]{:S(2)}) collective-permute-start(f32[224,256]{1,0:T(8,128)S(1)} %get-tuple-element.60), channel_id=1, source_target_pairs={{0,8},{8,16},{16,24},{1,9},{9,17},{17,25},{2,10},{10,18},{18,26},{... | collective-permute-start | bytes 688136 | tf_op jit(solution)/shard_map/ppermute | solution.py:427
  18.8 9.0 %collective-permute-start.3 = (f32[224,256]{1,0:T(8,128)S(1)}, f32[224,256]{1,0:T(8,128)S(1)}, u32[]{:S(2)}, u32[]{:S(2)}) collective-permute-start(f32[224,256]{1,0:T(8,128)S(1)} %get-tuple-element.61), channel_id=1, source_target_pairs={{8,0},{16,8},{24,16},{9,1},{17,9},{25,17},{10,2},{18,10},{26,18},{... | collective-permute-start | bytes 688136 | tf_op jit(solution)/shard_map/ppermute | solution.py:427
  20.2 6.6 %collective-permute-start.5 = (f32[264,128]{1,0:T(8,128)S(1)}, f32[264,128]{1,0:T(8,128)S(1)}, u32[]{:S(2)}, u32[]{:S(2)}) collective-permute-start(f32[264,128]{1,0:T(8,128)S(1)} %get-tuple-element.63), channel_id=1, source_target_pairs={{1,0},{2,1},{3,2},{4,3},{5,4},{6,5},{7,6},{9,8},{10,9},{11,10},{12... | collective-permute-start | bytes 405512 | tf_op jit(solution)/shard_map/ppermute | solution.py:427

commit v3 on v2

--- a/solution.py
+++ b/solution.py
@@ -27,18 +27,11 @@
     return lax.broadcasted_iota(I32, shape, dim)
 
 
-def split3(x):
+def pick(sel, x):
     hi = x.astype(BF16)
-    rest = x - hi.astype(F32)
-    mid = rest.astype(BF16)
-    low = (rest - mid.astype(F32)).astype(BF16)
-    return hi, mid, low
-
-
-def pick(sel, x):
-    hi, mid, low = split3(x)
+    mid = (x - hi.astype(F32)).astype(BF16)
     dot = functools.partial(jnp.dot, preferred_element_type=F32)
-    return (dot(sel, low) + dot(sel, mid)) + dot(sel, hi)
+    return dot(sel, mid) + dot(sel, hi)
 
 
 def hot(a, b):
@@ -55,16 +48,22 @@
     return jnp.take_along_axis(x, index, axis=1, mode="promise_in_bounds")
 
 
-def take_lanes(x, index):
-    low = index & 127
-    high = index >= 128
-    parts = []
+def take_lanes(xs, index):
+    columns = [[] for _ in xs]
     for t in (0, 1):
-        cut = slice(t * 128, (t + 1) * 128)
-        a = take128(x[:, :128], low[:, cut])
-        b = take128(x[:, 128:], low[:, cut])
-        parts.append(jnp.where(high[:, cut], b, a))
-    return jnp.concatenate(parts, axis=1)
+        cut = index[:, t * 128 : (t + 1) * 128]
+        low = cut & 127
+        high = cut > 127
+        rows = [[] for _ in xs]
+        for g in range(0, index.shape[0], 8):
+            at = slice(g, g + 8)
+            for x, row in zip(xs, rows, strict=True):
+                a = take128(x[at, :128], low[at])
+                b = take128(x[at, 128:], low[at])
+                row.append(jnp.where(high[at], b, a))
+        for column_parts, row in zip(columns, rows, strict=True):
+            column_parts.append(jnp.concatenate(row, axis=0))
+    return [jnp.concatenate(parts, axis=1) for parts in columns]
 
 
 def decode(far_line):
@@ -140,37 +139,34 @@
     return out
 
 
-def scatter(rows, node, xs, ys):
+def onehots(node, hots, work):
+    for t in (0, 1):
+        work[t, 0:SLOTS, :] = node[:, t * 128 : (t + 1) * 128].astype(F32)
+    places = iota((256, 256), 0).astype(F32).astype(BF16)
+    one, zero = jnp.ones((), BF16), jnp.zeros((), BF16)
+    for s in range(SLOTS):
+        row = jnp.concatenate([work[t, s : s + 1, :] for t in (0, 1)], axis=1)
+        index = jnp.broadcast_to(row.astype(BF16), (256, 256))
+        hots[s] = jnp.where(places == index, one, zero)
+
+
+def scatter(rows, hots, xs, ys):
     for r, value in enumerate(rows):
         for t in (0, 1):
             xs[t, pl.ds(r, SLOTS, stride=8), :] = value[:, t * 128 : (t + 1) * 128]
-    for t in (0, 1):
-        xs[t, pl.ds(4, SLOTS, stride=8), :] = node[:, t * 128 : (t + 1) * 128].astype(F32)
-        for r in [r for r in range(len(rows), 8) if r != 4]:
-            xs[t, pl.ds(r, SLOTS, stride=8), :] = jnp.zeros((SLOTS, 128), F32)
-    places = iota((256, 256), 0).astype(F32).astype(BF16)
-    one = jnp.ones((), BF16)
-    zero = jnp.zeros((), BF16)
-
-    def group(g, carry):
-        for i in range(8):
-            at = pl.multiple_of(g * 64 + i * 8, 8)
-            x = jnp.concatenate([xs[0, pl.ds(at, 8), :], xs[1, pl.ds(at, 8), :]], axis=1)
-            index = jnp.broadcast_to(x[4:5, :].astype(BF16), (256, 256))
-            onehot = jnp.where(places == index, one, zero)
-            hi = x.astype(BF16).astype(F32)
-            rest = x - hi
-            mid = rest.astype(BF16).astype(F32)
-            lhs = jnp.concatenate([hi, mid, rest - mid, jnp.zeros_like(x)], axis=0).astype(BF16)
-            got = lax.dot_general(
-                lhs, onehot, (((1,), (1,)), ((), ())), preferred_element_type=F32
-            )
-            total = (got[16:24] + got[8:16]) + got[0:8]
-            ys[0, pl.ds(at, 8), :] = total[:, :128]
-            ys[1, pl.ds(at, 8), :] = total[:, 128:]
-        return carry
-
-    lax.fori_loop(0, SLOTS // 8, group, 0)
+    for s in range(SLOTS):
+        at = slice(8 * s, 8 * s + 8)
+        x = jnp.concatenate([xs[0, at, :], xs[1, at, :]], axis=1)
+        hi = x.astype(BF16).astype(F32)
+        got = lax.dot_general(
+            jnp.concatenate([hi, x - hi], axis=0).astype(BF16),
+            hots[s],
+            (((1,), (1,)), ((), ())),
+            preferred_element_type=F32,
+        )
+        total = got[8:16] + got[0:8]
+        ys[0, at, :] = total[:, :128]
+        ys[1, at, :] = total[:, 128:]
     return [
         jnp.concatenate([ys[t, pl.ds(r, SLOTS, stride=8), :] for t in (0, 1)], axis=1)
         for r in range(len(rows))
@@ -179,7 +175,23 @@
 
 def pair_tile(first, second):
     lane = iota((8, 128), 1)
-    return jnp.where(lane == 0, first, jnp.where(lane == 1, second, 0.0))
+    return jnp.where(lane == 18, first, jnp.where(lane == 19, second, 0.0))
+
+
+def pack_edges(edges):
+    lane = iota((8, 128), 1)
+    out = jnp.zeros((8, 128), F32)
+    for g in range(4):
+        part = edges[8 * g : 8 * g + 8]
+        part = pltpu.roll(part, 32 * g, axis=1) if g else part
+        out = jnp.where((lane >= 32 * g) & (lane < 32 * g + 18), part, out)
+    return out
+
+
+def unpack_edges(tile):
+    return jnp.concatenate(
+        [tile] + [pltpu.roll(tile, 128 - 32 * g, axis=1) for g in range(1, 4)], axis=0
+    )
 
 
 def depth_of(gap, live):
@@ -190,19 +202,29 @@
     return jnp.sum(jnp.sum(x, axis=0, keepdims=True), axis=1, keepdims=True)
 
 
-def residual_of(near, pline):
+def first_mask(pline):
     shape = (SLOTS, SLOTS)
     row = jnp.broadcast_to(pline.astype(F32), shape)
     col = column(pline.astype(F32), 0, SLOTS)
     again = jnp.where((row == col) & (iota(shape, 1) < iota(shape, 0)), 1.0, 0.0)
     first = jnp.sum(again, axis=1, keepdims=True) == 0.0
+    return jnp.broadcast_to(jnp.where(first, 1.0, 0.0), (SLOTS, 256))
+
+
+def residual_of(near, first):
     square = near[0] * near[0] + near[1] * near[1] + near[2] * near[2]
-    return total2(jnp.where(first, square, 0.0))
-
-
-def respond(normal, energy, node, far, geom, pline, sel, requests, out, edge, change):
+    return total2(first[...] * square)
+
+
+def own_index(far):
+    z = far[...] - 3
+    return jnp.clip(z, 0, 255), (z >= 0) & (z < 256)
+
+
+def respond(normal, energy, node, far, geom, first, sel, requests, out, edge, change):
+    edge[...] = pack_edges(edge_lanes(normal, 0, 9))
     lines = [pick(sel[...], normal[c]) for c in range(3)]
-    residual = residual_of([v[0:SLOTS] for v in lines], pline)
+    residual = residual_of([v[0:SLOTS] for v in lines], first)
     tile = pair_tile(energy, residual)
     tile = jnp.concatenate([tile, tile], axis=1)
     for j in range(16):
@@ -210,35 +232,24 @@
         out[j, OUTER:24, :] = tile
     x, y, _ = position()
     me = x * 4 + y
-    for d, (buf, to, there) in enumerate(
-        (
-            (requests[0], me - 4, x > 0),
-            (requests[1], me + 4, x < 3),
-            (requests[2], me - 1, y > 0),
-            (requests[3], me + 1, y < 3),
-        )
-    ):
+    answers = []
+    for d, buf in enumerate(requests):
         at = 2 * SLOTS + OUTER * d
-        index = buf[192:208, :].astype(I32)
+        values = take_lanes([v[at : at + OUTER] for v in lines], buf[192:208, :].astype(I32))
         answer = jnp.zeros((OUTER, 256), F32)
         for c in range(3):
-            value = take_lanes(lines[c][at : at + OUTER], index)
-            answer = answer + buf[144 + 16 * c : 160 + 16 * c, :] * value
-
-        @pl.when(there)
-        def _():
-            out[jnp.where(there, to, 0), 0:OUTER, :] = answer
-
-    z = far[...] - 3
-    inside = (z >= 0) & (z < 256)
-    index = jnp.clip(z, 0, 255)
+            answer = answer + buf[144 + 16 * c : 160 + 16 * c, :] * values[c]
+        answers.append(answer)
+    index, inside = own_index(far)
+    near = take_lanes([v[0:SLOTS] for v in lines], node[...])
+    other = take_lanes([v[SLOTS : 2 * SLOTS] for v in lines], index)
     moved = jnp.zeros((SLOTS, 256), F32)
     for c in range(3):
-        near = take_lanes(lines[c][0:SLOTS], node[...])
-        other = jnp.where(inside, take_lanes(lines[c][SLOTS : 2 * SLOTS], index), 0.0)
-        moved = moved + geom[c] * (near - other)
+        moved = moved + geom[c] * (near[c] - jnp.where(inside, other[c], 0.0))
     change[...] = moved
-    edge[...] = edge_lanes(normal, 0, 9)
+    sides = ((me - 4, x > 0), (me + 4, x < 3), (me - 1, y > 0), (me + 1, y < 3))
+    for answer, (to, there) in zip(answers, sides, strict=True):
+        out[jnp.where(there, to, me), 0:OUTER, :] = answer
 
 
 def first_kernel(
@@ -264,6 +275,8 @@
     sel_out,
     selz_out,
     inverse_out,
+    hots,
+    first,
     xs,
     ys,
 ):
@@ -293,25 +306,25 @@
     edges = jnp.where(lane < 9, zhi[0:256, :], zlo[0:256, :])
     edges = pick(sel_pos[SLOTS + OUTER :], edges)
     ends = z_values(edges, far[OUTER:, :])
-    z = far[...] - 3
-    within = (z >= 0) & (z < 256)
-    index = jnp.clip(z, 0, 255)
+    index, within = own_index(far)
     gap = -geom[3]
     terms = jnp.zeros((SLOTS, 256), F32)
     for c in range(3):
         got = pick(sel_pos, pos[c])
         faces = jnp.concatenate([buf[48 * c : 48 * c + 48, :] for buf in requests], axis=0)
         outer = got[SLOTS + OUTER :] + pick(sel_face, faces)
-        near = take_lanes(got[0:SLOTS], node[...])
+        (near,) = take_lanes([got[0:SLOTS]], node[...])
         other = jnp.concatenate([got[SLOTS : SLOTS + OUTER], outer], axis=0)
-        other = jnp.where(within, take_lanes(other, index), 0.0)
+        other = jnp.where(within, take_lanes([other], index)[0], 0.0)
         other = other + jnp.concatenate([jnp.zeros((OUTER, 256), F32), ends[c]], axis=0)
         terms = terms + geom[c] * (near - other)
     gap = terms + gap
     gap_out[...] = gap
+    onehots(node, hots, xs)
+    first[...] = first_mask(pline[...])
     depth = depth_of(gap, live[...])
     ones = jnp.where(iota((SLOTS, 256), 0) < live[...], 1.0, 0.0)
-    got = scatter([depth * geom[c] for c in range(3)] + [ones], node[...], xs, ys)
+    got = scatter([depth * geom[c] for c in range(3)] + [ones], hots, xs, ys)
     inverse = 1.0 / (1.0 + pick(sel[0:SLOTS], got[3]))
     inverse_out[...] = inverse
     normal = [got[c] * inverse for c in range(3)]
@@ -319,21 +332,22 @@
         normal_out[c] = normal[c]
         moved_out[c] = jnp.zeros((SLOTS, 256), F32)
     respond(
-        normal, total2(depth * depth), node, far, geom, pline[...], sel_out, requests, out, edge,
+        normal, total2(depth * depth), node, far, geom, first, sel_out, requests, out, edge,
         change,
     )
 
 
 def forward_kernel(got, edge, out):
     sums = jnp.sum(got[:, OUTER:24, 0:128], axis=0)
+    lane = iota((8, 128), 1)
+    sums = jnp.where((iota((8, 128), 0) == 0) & (lane > 17) & (lane < 20), sums, edge[...])
     for j in range(8):
-        out[j, 0:SLOTS, :] = edge[...]
-        out[j, SLOTS:40, :] = sums
+        out[j] = sums
 
 
 def update(gap, change, far, geom, got, gotz, selz):
-    sums = jnp.sum(gotz[:, SLOTS:40, :], axis=0)
-    energy = sums[0:1, 0:1]
+    sums = jnp.sum(gotz[...], axis=0)
+    energy = sums[0:1, 18:19]
     scale = RELAX * (1.0 / (1.0 + energy / N_PAIRS))
     x, y, k = position()
     me = x * 4 + y
@@ -342,8 +356,10 @@
         reply = got[jnp.where(there, to, me), 0:OUTER, :]
         outer = outer + jnp.where(there, reply, 0.0)
     lane = iota((SLOTS, 128), 1)
-    above = jnp.where((lane < 9) & (k < 7), gotz[jnp.minimum(k + 1, 7), 0:SLOTS, :], 0.0)
-    below = jnp.where((lane >= 9) & (k > 0), gotz[jnp.maximum(k - 1, 0), 0:SLOTS, :], 0.0)
+    above = unpack_edges(gotz[jnp.minimum(k + 1, 7)])
+    above = jnp.where((lane < 9) & (k < 7), above, 0.0)
+    below = unpack_edges(gotz[jnp.maximum(k - 1, 0)])
+    below = jnp.where((lane > 8) & (lane < 18) & (k > 0), below, 0.0)
     ends = z_values(
         pick(selz[...], jnp.concatenate([above, below], axis=0)), far[OUTER:, :]
     )
@@ -354,7 +370,7 @@
 
 
 def sweep_kernel(
-    last, gap, change, normal, moved, inverse, node, far, geom, pline, live, sel, selz,
+    last, gap, change, normal, moved, inverse, node, far, geom, first, live, sel, selz, hots,
     got, gotz, *rest,
 ):
     if last:
@@ -368,18 +384,18 @@
         moved_out[c] = moved[c] + scale * normal[c]
     depth = depth_of(fresh, live[...])
     energy = total2(depth * depth)
-    found = scatter([depth * geom[c] for c in range(3)], node[...], xs, ys)
+    found = scatter([depth * geom[c] for c in range(3)], hots, xs, ys)
     fresh_normal = [found[c] * inverse[...] for c in range(3)]
     for c in range(3):
         normal_out[c] = fresh_normal[c]
     if last:
         lines = [pick(sel[0:SLOTS, :], fresh_normal[c]) for c in range(3)]
-        tile = pair_tile(energy, residual_of(lines, pline[...]))
+        tile = pair_tile(energy, residual_of(lines, first))
         out[...] = jnp.broadcast_to(tile[0:1, :], (128, 128))
     else:
         gap_out[...] = fresh
         respond(
-            fresh_normal, energy, node, far, geom, pline[...], sel, (xlo, xhi, ylo, yhi), out, edge,
+            fresh_normal, energy, node, far, geom, first, sel, (xlo, xhi, ylo, yhi), out, edge,
             change_out,
         )
 
@@ -387,13 +403,13 @@
 def last_kernel(pos, normal, moved, pline, got, s0, s1, s2, s3, out, history):
     sums = jnp.sum(got[...], axis=0, keepdims=True)
     every = [s[0:1, :] for s in (s0, s1, s2, s3)] + [sums]
-    scales = [RELAX * (1.0 / (1.0 + s[:, 0:1] / N_PAIRS)) for s in every]
+    scales = [RELAX * (1.0 / (1.0 + s[:, 18:19] / N_PAIRS)) for s in every]
     sel = hot(iota((256, SLOTS), 0), jnp.broadcast_to(pline[...], (256, SLOTS)))
     for c in range(3):
         out[c] = pos[c] + pick(sel, moved[c] + scales[-1] * normal[c])
     for t in range(SWEEPS):
-        residual = scales[t] * scales[t] * every[t][:, 1:2]
-        history[0:1, t : t + 1] = jnp.sqrt(1.0 + every[t][:, 0:1] / PAIRS_SLOTS)
+        residual = scales[t] * scales[t] * every[t][:, 19:20]
+        history[0:1, t : t + 1] = jnp.sqrt(1.0 + every[t][:, 18:19] / PAIRS_SLOTS)
         history[1:2, t : t + 1] = jnp.sqrt(1.0 + residual / NODES_BLK)
 
 
@@ -460,8 +476,8 @@
     zlo = shift(zup, GZ, True)
     zhi = shift(zdn, GZ, False)
     triple = shape(3, SLOTS, 256)
-    outbound, edges = shape(16, 24, 256), shape(SLOTS, 128)
-    out, edge, change, gap, normal, moved, sel, selz, inverse = call(
+    outbound, edges = shape(16, 24, 256), shape(8, 128)
+    out, edge, change, gap, normal, moved, sel, selz, inverse, hots, first = call(
         first_kernel,
         [
             outbound,
@@ -473,6 +489,8 @@
             shape(128, SLOTS, dtype=BF16),
             shape(OUTER, 2 * SLOTS, dtype=BF16),
             flat,
+            shape(SLOTS, 256, 256, dtype=BF16),
+            flat,
         ],
         [pos, node, far, geom, pline, fline, live, *requests, zlo, zhi],
         work,
@@ -480,12 +498,12 @@
     totals = []
     for t in range(1, SWEEPS):
         got = lax.all_to_all(out, XY, 0, 0, tiled=True)
-        out = call(forward_kernel, shape(8, 40, 128), [got, edge])
+        out = call(forward_kernel, shape(8, 8, 128), [got, edge])
         gotz = lax.all_to_all(out, GZ, 0, 0, tiled=True)
         last = t + 1 == SWEEPS
         args = [
-            gap, change, normal, moved, inverse, node, far, geom, pline, live, sel, selz,
-            got, gotz,
+            gap, change, normal, moved, inverse, node, far, geom, first, live, sel, selz,
+            hots, got, gotz,
         ]
         sums_shape = shape(8, 128)
         if last:

time: 156 us -> 147 us (0.942)
  Pallas kernels: 21.3 us -> 15.9 us
  blocking collectives: 106 us -> 103 us
    pallas_call x11, Pallas kernels: 21.3 us -> 15.9 us  [call(): pl.pallas_call(kernel, out_shape=outs, in_specs=[vmem] * len(args), out_s...]
    all_to_all x4, blocking collectives: 40.4 us -> 36.5 us  [local(): gotz = lax.all_to_all(out, GZ, 0, 0, tiled=True)]
where the time goes in v3:
time: 147 us
  blocking collectives  103 us (70%)
  Pallas kernels  15.9 us (11%)
  starting transfers between devices  15.8 us (11%)
  waiting for transfers between devices  5.8 us (4%)
  local copies, waits for them, and re-layouts  4.85 us (3%)
    all_to_all x4, blocking collectives, local(): got = lax.all_to_all(out, XY, 0, 0, tiled=True)  53 us
    all_to_all x4, blocking collectives, local(): gotz = lax.all_to_all(out, GZ, 0, 0, tiled=True)  36.5 us
    pallas_call x11, Pallas kernels, call(): pl.pallas_call(kernel, out_shape=outs, in_specs=[vmem] * len(args), out_s...  15.9 us
    ppermute x6, starting transfers between devices, shift(): return lax.ppermute(x, axis, pairs if up else [(b, a) for a, b in pairs])  15.8 us
    all_to_all x1, blocking collectives, local(): got = lax.all_to_all(out, ALL, 0, 0, tiled=True)  13.4 us
    ppermute x6, waiting for transfers between devices, shift(): return lax.ppermute(x, axis, pairs if up else [(b, a) for a, b in pairs])  5.8 us
    unnamed x12, local copies, waits for them, and re-layouts  4.85 us
  transfers between devices with their start and end apart: 6, of which 2 were waited for; matrix products, arithmetic and copies ran while one was open for 0% of the time, Pallas kernels for 0%

profile of v3, /device:TPU:1, one launch (start us, length us, event | category | flops | bytes accessed | tf_op | source)
XLA Modules:
  0.0 146.5 jit_solution(14977274506738670416)
XLA Ops:
  1.3 0.0 copy-start
  1.3 1.1 copy-done
  2.4 0.0 copy-start.1
  2.4 0.9 copy-done.1
  3.3 0.0 copy-start.2
  3.3 0.8 copy-done.2
  4.1 0.0 copy-start.3
  4.1 0.8 copy-done.3
  4.8 0.0 copy-start.4
  4.8 0.7 copy-done.4
  5.5 0.0 copy-start.5
  5.5 0.7 copy-done.5
  6.1 0.8 shard_map.86
  6.9 4.5 %collective-permute-start.4 = (f32[264,128]{1,0:T(8,128)S(1)}, f32[264,128]{1,0:T(8,128)S(1)}, u32[]{:S(2)}, u32[]{:S(2)}) collective-permute-start(f32[264,128]{1,0:T(8,128)S(1)} %get-tuple-element.64), channel_id=1, source_target_pairs={{0,1},{1,2},{2,3},{3,4},{4,5},{5,6},{6,7},{8,9},{9,10},{10,11},{11... | collective-permute-start | bytes 405512 | tf_op jit(solution)/shard_map/ppermute | solution.py:443
  11.4 3.6 %collective-permute-start = (f32[224,256]{1,0:T(8,128)S(1)}, f32[224,256]{1,0:T(8,128)S(1)}, u32[]{:S(2)}, u32[]{:S(2)}) collective-permute-start(f32[224,256]{1,0:T(8,128)S(1)} %get-tuple-element.60), channel_id=1, source_target_pairs={{0,32},{32,64},{64,96},{1,33},{33,65},{65,97},{2,34},{34,66},{66,9... | collective-permute-start | bytes 688136 | tf_op jit(solution)/shard_map/ppermute | solution.py:443
  15.0 1.3 collective-permute-start.1
  16.3 3.2 %collective-permute-start.2 = (f32[224,256]{1,0:T(8,128)S(1)}, f32[224,256]{1,0:T(8,128)S(1)}, u32[]{:S(2)}, u32[]{:S(2)}) collective-permute-start(f32[224,256]{1,0:T(8,128)S(1)} %get-tuple-element.62), channel_id=1, source_target_pairs={{0,8},{8,16},{16,24},{1,9},{9,17},{17,25},{2,10},{10,18},{18,26},{... | collective-permute-start | bytes 688136 | tf_op jit(solution)/shard_map/ppermute | solution.py:443
  19.5 1.3 collective-permute-start.3
  20.8 0.0 collective-permute-done.4.zlo
  20.8 1.9 %collective-permute-start.5 = (f32[264,128]{1,0:T(8,128)S(1)}, f32[264,128]{1,0:T(8,128)S(1)}, u32[]{:S(2)}, u32[]{:S(2)}) collective-permute-start(f32[264,128]{1,0:T(8,128)S(1)} %get-tuple-element.65), channel_id=1, source_target_pairs={{1,0},{2,1},{3,2},{4,3},{5,4},{6,5},{7,6},{9,8},{10,9},{11,10},{12... | collective-permute-start | bytes 405512 | tf_op jit(solution)/shard_map/ppermute | solution.py:443
  22.7 4.7 %collective-permute-done.5.zhi = f32[264,128]{1,0:T(8,128)S(1)} collective-permute-done((f32[264,128]{1,0:T(8,128)S(1)}, f32[264,128]{1,0:T(8,128)S(1)}, u32[]{:S(2)}, u32[]{:S(2)}) %collective-permute-start.5) | collective-permute-done | bytes 135200 | tf_op jit(solution)/shard_map/ppermute | solution.py:443
  27.4 0.0 collective-permute-done.xlo.rest_0_
  27.4 0.0 collective-permute-done.1.xhi.rest_1_
  27.4 0.0 collective-permute-done.2.ylo.rest_2_
  27.4 1.1 collective-permute-done.3.yhi.rest_3_
  28.5 3.4 %shard_map.87 = (f32[16,24,256]{2,1,0:T(8,128)S(1)}, f32[8,128]{1,0:T(8,128)S(1)}, f32[32,256]{1,0:T(8,128)S(1)}, f32[32,256]{1,0:T(8,128)S(1)}, f32[3,32,256]{2...) custom-call(f32[3,256,256]{2,1,0:T(8,128)S(1)} %get-tuple-element.53, ...), custom_call_target="tpu_custom_call" | custom-call | tf_op jit(solution)/shard_map/pallas_call | solution.py:422
  31.9 17.6 %all_to_all.51.got = f32[16,24,256]{2,1,0:T(8,128)S(1)} all-to-all(f32[16,24,256]{2,1,0:T(8,128)S(1)} %get-tuple-element.75), channel_id=1, replica_groups=mesh['gx'=4,'gy'=4,'gz_0'=4,'gz_1'=2] {'gx','gy'}, dimensions={0} | all-to-all | bytes 786432 | tf_op jit(solution)/shard_map/all_to_all | solution.py:500
  49.5 9.7 %all_to_all.52.gotz = f32[8,8,128]{2,1,0:T(8,128)S(1)} all-to-all(f32[8,8,128]{2,1,0:T(8,128)S(1)} %shard_map.88), channel_id=1, replica_groups=mesh['gx'=4,'gy'=4,'gz_0'=4,'gz_1'=2] {'gz_0','gz_1'}, dimensions={0} | all-to-all | bytes 65536 | tf_op jit(solution)/shard_map/all_to_all | solution.py:502
  59.2 2.7 %shard_map.89 = (f32[16,24,256]{2,1,0:T(8,128)S(1)}, f32[8,128]{1,0:T(8,128)S(1)}, f32[32,256]{1,0:T(8,128)S(1)}, f32[32,256]{1,0:T(8,128)S(1)}, f32[8,128]{1,0:...) custom-call(f32[32,256]{1,0:T(8,128)S(1)} %get-tuple-element.66.gap, ...), custom_call_target="tpu_custom_call" | custom-call | tf_op jit(solution)/shard_map/pallas_call | solution.py:422
  61.9 11.8 %all_to_all.53.got = f32[16,24,256]{2,1,0:T(8,128)S(1)} all-to-all(f32[16,24,256]{2,1,0:T(8,128)S(1)} %get-tuple-element.81), channel_id=1, replica_groups=mesh['gx'=4,'gy'=4,'gz_0'=4,'gz_1'=2] {'gx','gy'}, dimensions={0} | all-to-all | bytes 786432 | tf_op jit(solution)/shard_map/all_to_all | solution.py:500
  73.7 9.0 %all_to_all.54.gotz = f32[8,8,128]{2,1,0:T(8,128)S(1)} all-to-all(f32[8,8,128]{2,1,0:T(8,128)S(1)} %shard_map.90), channel_id=1, replica_groups=mesh['gx'=4,'gy'=4,'gz_0'=4,'gz_1'=2] {'gz_0','gz_1'}, dimensions={0} | all-to-all | bytes 65536 | tf_op jit(solution)/shard_map/all_to_all | solution.py:502
  82.7 2.7 %shard_map.91 = (f32[16,24,256]{2,1,0:T(8,128)S(1)}, f32[8,128]{1,0:T(8,128)S(1)}, f32[32,256]{1,0:T(8,128)S(1)}, f32[32,256]{1,0:T(8,128)S(1)}, f32[8,128]{1,0:...) custom-call(f32[32,256]{1,0:T(8,128)S(1)} %get-tuple-element.77.gap, ...), custom_call_target="tpu_custom_call" | custom-call | tf_op jit(solution)/shard_map/pallas_call | solution.py:422
  85.4 11.8 %all_to_all.55.got = f32[16,24,256]{2,1,0:T(8,128)S(1)} all-to-all(f32[16,24,256]{2,1,0:T(8,128)S(1)} %get-tuple-element.87), channel_id=1, replica_groups=mesh['gx'=4,'gy'=4,'gz_0'=4,'gz_1'=2] {'gx','gy'}, dimensions={0} | all-to-all | bytes 786432 | tf_op jit(solution)/shard_map/all_to_all | solution.py:500
  97.2 9.0 %all_to_all.56.gotz = f32[8,8,128]{2,1,0:T(8,128)S(1)} all-to-all(f32[8,8,128]{2,1,0:T(8,128)S(1)} %shard_map.92), channel_id=1, replica_groups=mesh['gx'=4,'gy'=4,'gz_0'=4,'gz_1'=2] {'gz_0','gz_1'}, dimensions={0} | all-to-all | bytes 65536 | tf_op jit(solution)/shard_map/all_to_all | solution.py:502
  106.1 2.7 %shard_map.93 = (f32[16,24,256]{2,1,0:T(8,128)S(1)}, f32[8,128]{1,0:T(8,128)S(1)}, f32[32,256]{1,0:T(8,128)S(1)}, f32[32,256]{1,0:T(8,128)S(1)}, f32[8,128]{1,0:...) custom-call(f32[32,256]{1,0:T(8,128)S(1)} %get-tuple-element.83.gap, ...), custom_call_target="tpu_custom_call" | custom-call | tf_op jit(solution)/shard_map/pallas_call | solution.py:422
  108.9 11.8 %all_to_all.57.got = f32[16,24,256]{2,1,0:T(8,128)S(1)} all-to-all(f32[16,24,256]{2,1,0:T(8,128)S(1)} %get-tuple-element.93), channel_id=1, replica_groups=mesh['gx'=4,'gy'=4,'gz_0'=4,'gz_1'=2] {'gx','gy'}, dimensions={0} | all-to-all | bytes 786432 | tf_op jit(solution)/shard_map/all_to_all | solution.py:500
  120.7 9.0 %all_to_all.58.gotz = f32[8,8,128]{2,1,0:T(8,128)S(1)} all-to-all(f32[8,8,128]{2,1,0:T(8,128)S(1)} %shard_map.94), channel_id=1, replica_groups=mesh['gx'=4,'gy'=4,'gz_0'=4,'gz_1'=2] {'gz_0','gz_1'}, dimensions={0} | all-to-all | bytes 65536 | tf_op jit(solution)/shard_map/all_to_all | solution.py:502
  129.6 2.2 %shard_map.95 = (f32[128,128]{1,0:T(8,128)S(1)}, f32[8,128]{1,0:T(8,128)S(1)}, f32[3,32,256]{2,1,0:T(8,128)S(1)}, f32[3,32,256]{2,1,0:T(8,128)S(1)}) custom-call(f32[32,256]{1,0:T(8,128)S(1)} %get-tuple-element.89.gap, f32[32,256]{1,0:T(8,128)S(1)} %get-tuple-element.90.change, f32[3,32,256]{2,1,0:T(8,128)S(1)} %get-tuple-element.91.normal, ...), custom_call_target="tpu_custom_call" | custom-call | tf_op jit(solution)/shard_map/pallas_call | solution.py:422
  131.9 13.4 %all_to_all.59 = f32[128,1,128]{2,1,0:T(1,128)S(1)} all-to-all(f32[128,1,128]{2,1,0:T(1,128)S(1)} %bitcast.16), channel_id=1, replica_groups=mesh['gx'=4,'gy'=4,'gz_0'=4,'gz_1'=2] {'gx','gy','gz_0','gz_1'}, dimensions={0} | all-to-all | bytes 131072 | tf_op jit(solution)/shard_map/all_to_all | solution.py:524
  145.2 1.3 shard_map.96
  (4 shorter events, 0.1 us)
Async XLA Ops:
  1.3 1.1 copy-start
  2.4 0.9 copy-start.1
  3.3 0.8 copy-start.2
  4.1 0.8 copy-start.3
  4.8 0.7 copy-start.4
  5.5 0.7 copy-start.5
  6.9 13.9 %collective-permute-start.4 = (f32[264,128]{1,0:T(8,128)S(1)}, f32[264,128]{1,0:T(8,128)S(1)}, u32[]{:S(2)}, u32[]{:S(2)}) collective-permute-start(f32[264,128]{1,0:T(8,128)S(1)} %get-tuple-element.64), channel_id=1, source_target_pairs={{0,1},{1,2},{2,3},{3,4},{4,5},{5,6},{6,7},{8,9},{9,10},{10,11},{11... | collective-permute-start | bytes 405512 | tf_op jit(solution)/shard_map/ppermute | solution.py:443
  11.4 16.0 %collective-permute-start = (f32[224,256]{1,0:T(8,128)S(1)}, f32[224,256]{1,0:T(8,128)S(1)}, u32[]{:S(2)}, u32[]{:S(2)}) collective-permute-start(f32[224,256]{1,0:T(8,128)S(1)} %get-tuple-element.60), channel_id=1, source_target_pairs={{0,32},{32,64},{64,96},{1,33},{33,65},{65,97},{2,34},{34,66},{66,9... | collective-permute-start | bytes 688136 | tf_op jit(solution)/shard_map/ppermute | solution.py:443
  15.0 12.5 %collective-permute-start.1 = (f32[224,256]{1,0:T(8,128)S(1)}, f32[224,256]{1,0:T(8,128)S(1)}, u32[]{:S(2)}, u32[]{:S(2)}) collective-permute-start(f32[224,256]{1,0:T(8,128)S(1)} %get-tuple-element.61), channel_id=1, source_target_pairs={{32,0},{64,32},{96,64},{33,1},{65,33},{97,65},{34,2},{66,34},{98,6... | collective-permute-start | bytes 688136 | tf_op jit(solution)/shard_map/ppermute | solution.py:443
  16.3 11.2 %collective-permute-start.2 = (f32[224,256]{1,0:T(8,128)S(1)}, f32[224,256]{1,0:T(8,128)S(1)}, u32[]{:S(2)}, u32[]{:S(2)}) collective-permute-start(f32[224,256]{1,0:T(8,128)S(1)} %get-tuple-element.62), channel_id=1, source_target_pairs={{0,8},{8,16},{16,24},{1,9},{9,17},{17,25},{2,10},{10,18},{18,26},{... | collective-permute-start | bytes 688136 | tf_op jit(solution)/shard_map/ppermute | solution.py:443
  19.5 9.0 %collective-permute-start.3 = (f32[224,256]{1,0:T(8,128)S(1)}, f32[224,256]{1,0:T(8,128)S(1)}, u32[]{:S(2)}, u32[]{:S(2)}) collective-permute-start(f32[224,256]{1,0:T(8,128)S(1)} %get-tuple-element.63), channel_id=1, source_target_pairs={{8,0},{16,8},{24,16},{9,1},{17,9},{25,17},{10,2},{18,10},{26,18},{... | collective-permute-start | bytes 688136 | tf_op jit(solution)/shard_map/ppermute | solution.py:443
  20.8 6.6 %collective-permute-start.5 = (f32[264,128]{1,0:T(8,128)S(1)}, f32[264,128]{1,0:T(8,128)S(1)}, u32[]{:S(2)}, u32[]{:S(2)}) collective-permute-start(f32[264,128]{1,0:T(8,128)S(1)} %get-tuple-element.65), channel_id=1, source_target_pairs={{1,0},{2,1},{3,2},{4,3},{5,4},{6,5},{7,6},{9,8},{10,9},{11,10},{12... | collective-permute-start | bytes 405512 | tf_op jit(solution)/shard_map/ppermute | solution.py:443

commit v4 on v3

--- a/solution.py
+++ b/solution.py
@@ -88,22 +88,62 @@
     return out
 
 
+def pack_rows(tall):
+    lane = iota((SLOTS, 128), 1)
+    out = jnp.zeros((SLOTS, 128), F32)
+    for g in range(8):
+        part = tall[32 * g : 32 * g + 32]
+        part = pltpu.roll(part, 16 * g, axis=1) if g else part
+        out = jnp.where((lane >= 16 * g) & (lane < 16 * g + 16), part, out)
+    return out
+
+
+def unpack_rows(flat):
+    return jnp.concatenate(
+        [flat] + [pltpu.roll(flat, 128 - 16 * g, axis=1) for g in range(1, 8)], axis=0
+    )
+
+
 def pack_kernel(
-    pos, node, far, geom, pline, fline, live, xdn, xup, ydn, yup, zdn, zup, geom_out, *copies
+    pos_in, node_in, far_in, geom_in, pline_in, fline_in, live_in,
+    xdn, xup, ydn, yup, zdn, zup, geom, pos, node, far, pline, fline, live,
+    geom_raw, sems,
 ):
-    for source, copy in zip((pos, node, far, pline, fline, live), copies, strict=True):
-        copy[...] = source[...]
+    copies = [
+        pltpu.make_async_copy(source, target, sems.at[n])
+        for n, (source, target) in enumerate(
+            (
+                (fline_in, fline),
+                (far_in, far),
+                (geom_in, geom_raw),
+                (pline_in, pline),
+                (pos_in, pos),
+                (node_in, node),
+                (live_in, live),
+            )
+        )
+    ]
+    for copy in copies:
+        copy.start()
+    for copy in copies[:4]:
+        copy.wait()
     for c in range(4):
-        geom_out[c] = geom[:, c, :]
+        geom[c] = geom_raw[:, c, :]
     fcol = column(fline[...].astype(F32), OUTER, OUTER).astype(I32)
     x, y, line = decode(fcol)
     tag = (line + 1).astype(F32)
     far_z = jnp.clip(far[OUTER:, :] - 3, 0, 255).astype(F32)
     for buf, mask in ((xdn, x < 0), (xup, x > 15), (ydn, y < 0), (yup, y > 15)):
         for c in range(3):
-            buf[144 + 16 * c : 160 + 16 * c, :] = geom_out[c, OUTER:, :]
+            buf[144 + 16 * c : 160 + 16 * c, :] = geom[c, OUTER:, :]
         buf[192:208, :] = far_z
         buf[208:224, :] = jnp.broadcast_to(jnp.where(mask, tag, 0.0), (OUTER, 256))
+    lines = jnp.broadcast_to(pline[...].astype(F32) + 1.0, (8, SLOTS))
+    for buf in (zdn, zup):
+        buf[32:40, :] = jnp.zeros((8, 128), F32)
+        buf[32:40, 0:SLOTS] = lines
+    for copy in copies[4:]:
+        copy.wait()
     for c in range(3):
         xdn[48 * c : 48 * c + 48, :] = pos[c, 0:48, :]
         xup[48 * c : 48 * c + 48, :] = pos[c, 208:256, :]
@@ -112,12 +152,8 @@
             ydn[to : to + 3, :] = pos[c, 16 * i : 16 * i + 3, :]
             yup[to : to + 3, :] = pos[c, 16 * i + 13 : 16 * i + 16, :]
     parts = [pos[c] for c in range(3)]
-    zdn[0:256, :] = edge_lanes(parts, 0, None)
-    zup[0:256, :] = edge_lanes(parts, None, 9)
-    lines = jnp.broadcast_to(pline[...].astype(F32) + 1.0, (8, SLOTS))
-    for buf in (zdn, zup):
-        buf[256:264, :] = jnp.zeros((8, 128), F32)
-        buf[256:264, 0:SLOTS] = lines
+    zdn[0:32, :] = pack_rows(edge_lanes(parts, 0, None))
+    zup[0:32, :] = pack_rows(edge_lanes(parts, None, 0))
 
 
 def z_index(far_outer):
@@ -226,10 +262,9 @@
     lines = [pick(sel[...], normal[c]) for c in range(3)]
     residual = residual_of([v[0:SLOTS] for v in lines], first)
     tile = pair_tile(energy, residual)
-    tile = jnp.concatenate([tile, tile], axis=1)
     for j in range(16):
-        out[j, 0:OUTER, :] = jnp.zeros((OUTER, 256), F32)
-        out[j, OUTER:24, :] = tile
+        out[j, 0:32, :] = jnp.zeros((32, 128), F32)
+        out[j, 32:40, :] = tile
     x, y, _ = position()
     me = x * 4 + y
     answers = []
@@ -249,85 +284,81 @@
     change[...] = moved
     sides = ((me - 4, x > 0), (me + 4, x < 3), (me - 1, y > 0), (me + 1, y < 3))
     for answer, (to, there) in zip(answers, sides, strict=True):
-        out[jnp.where(there, to, me), 0:OUTER, :] = answer
-
-
-def first_kernel(
-    pos,
-    node,
-    far,
-    geom,
-    pline,
-    fline,
-    live,
-    xlo,
-    xhi,
-    ylo,
-    yhi,
-    zlo,
-    zhi,
-    out,
-    edge,
-    change,
-    gap_out,
-    normal_out,
-    moved_out,
-    sel_out,
-    selz_out,
-    inverse_out,
-    hots,
-    first,
-    xs,
-    ys,
+        out[jnp.where(there, to, me), 0:OUTER, :] = answer[:, :128]
+        out[jnp.where(there, to, me), OUTER:32, :] = answer[:, 128:]
+
+
+def base_kernel(
+    pos, node, far, geom, pline, fline, live,
+    gap_out, own_out, face_out, inverse_out, hots, first, xs, ys,
 ):
+    onehots(node, hots, xs)
+    first[...] = first_mask(pline[...])
     own = pline[...].astype(F32)
     near_col = column(own, 0, SLOTS)
     far_col = column(fline[...].astype(F32), 0, SLOTS)
     x, y, line = decode(far_col.astype(I32))
     inside = (x >= 0) & (x < 16) & (y >= 0) & (y < 16)
     local = jnp.where(inside, line, -2).astype(F32)
+    both = jnp.concatenate([near_col, local], axis=0)
+    own_out[...] = jnp.broadcast_to(both, (2 * SLOTS, 128))
     xo, yo = x[OUTER:], y[OUTER:]
     face = jnp.where(xo < 0, (xo + 3) * 16 + yo, -1)
     face = jnp.where(xo > 15, 48 + (xo - 16) * 16 + yo, face)
     face = jnp.where(yo < 0, 96 + xo * 3 + yo + 3, face)
     face = jnp.where(yo > 15, 144 + xo * 3 + yo - 16, face)
+    face_out[...] = hot(iota((OUTER, 192), 1), face)
+    ones = jnp.where(iota((SLOTS, 256), 0) < live[...], 1.0, 0.0)
+    (counts,) = scatter([ones], hots, xs, ys)
+    same = hot(jnp.broadcast_to(own, (SLOTS, SLOTS)), near_col)
+    inverse_out[...] = 1.0 / (1.0 + pick(same, counts))
+    sel = hot(iota((2 * SLOTS, 256), 1).astype(F32), both)
+    index, within = own_index(far)
+    got = [pick(sel, pos[c]) for c in range(3)]
+    near = take_lanes([v[0:SLOTS] for v in got], node[...])
+    other = take_lanes([v[SLOTS:] for v in got], index)
+    gap = jnp.zeros((SLOTS, 256), F32)
+    for c in range(3):
+        gap = gap + geom[c] * (near[c] - jnp.where(within, other[c], 0.0))
+    gap_out[...] = gap - geom[3]
+
+
+def first_kernel(
+    gap_in, own, face, inverse, far, geom, pline, live, node, hots, first,
+    xlo, xhi, ylo, yhi, zlo, zhi,
+    out, edge, change, gap_out, normal_out, moved_out, sel_out, selz_out, xs, ys,
+):
     requests = (xlo, xhi, ylo, yhi)
     wanted = jnp.concatenate(
-        [near_col, local] + [buf[208:224, 0:1] - 1.0 for buf in requests], axis=0
-    )
-    sel = hot(jnp.broadcast_to(own, (128, SLOTS)), wanted)
-    sel_out[...] = sel
-    selz = jnp.concatenate([zhi[256:257, 0:SLOTS], zlo[256:257, 0:SLOTS]], axis=1) - 1.0
-    selz_out[...] = hot(jnp.broadcast_to(selz, (OUTER, 2 * SLOTS)), local[OUTER:])
-    lines_f = iota((2 * SLOTS, 256), 1).astype(F32)
-    sel_pos = hot(lines_f, jnp.concatenate([near_col, local], axis=0))
-    sel_face = hot(iota((OUTER, 192), 1), face)
-    lane = iota((256, 128), 1)
-    edges = jnp.where(lane < 9, zhi[0:256, :], zlo[0:256, :])
-    edges = pick(sel_pos[SLOTS + OUTER :], edges)
-    ends = z_values(edges, far[OUTER:, :])
+        [own[:, 0:1]] + [buf[208:224, 0:1] - 1.0 for buf in requests], axis=0
+    )
+    sel_out[...] = hot(jnp.broadcast_to(pline[...].astype(F32), (128, SLOTS)), wanted)
+    local = own[SLOTS + OUTER :, 0:1]
+    selz = jnp.concatenate([zhi[32:33, 0:SLOTS], zlo[32:33, 0:SLOTS]], axis=1) - 1.0
+    selz_out[...] = hot(jnp.broadcast_to(selz, (OUTER, 2 * SLOTS)), local)
+    edges = jnp.where(
+        iota((256, 128), 1) < 9,
+        unpack_rows(zhi[0:32, :]),
+        pltpu.roll(unpack_rows(zlo[0:32, :]), 9, axis=1),
+    )
+    sel = hot(iota((OUTER, 256), 1).astype(F32), local)
+    ends = z_values(pick(sel, edges), far[OUTER:, :])
     index, within = own_index(far)
-    gap = -geom[3]
-    terms = jnp.zeros((SLOTS, 256), F32)
-    for c in range(3):
-        got = pick(sel_pos, pos[c])
-        faces = jnp.concatenate([buf[48 * c : 48 * c + 48, :] for buf in requests], axis=0)
-        outer = got[SLOTS + OUTER :] + pick(sel_face, faces)
-        (near,) = take_lanes([got[0:SLOTS]], node[...])
-        other = jnp.concatenate([got[SLOTS : SLOTS + OUTER], outer], axis=0)
-        other = jnp.where(within, take_lanes([other], index)[0], 0.0)
-        other = other + jnp.concatenate([jnp.zeros((OUTER, 256), F32), ends[c]], axis=0)
-        terms = terms + geom[c] * (near - other)
-    gap = terms + gap
+    faces = [
+        pick(face[...], jnp.concatenate([buf[48 * c : 48 * c + 48, :] for buf in requests], axis=0))
+        for c in range(3)
+    ]
+    faces = take_lanes(faces, index[OUTER:])
+    outer = jnp.zeros((OUTER, 256), F32)
+    for c in range(3):
+        outer = outer + geom[c, OUTER:, :] * (
+            jnp.where(within[OUTER:], faces[c], 0.0) + ends[c]
+        )
+    gap = gap_in[...] - jnp.concatenate([jnp.zeros((OUTER, 256), F32), outer], axis=0)
     gap_out[...] = gap
-    onehots(node, hots, xs)
-    first[...] = first_mask(pline[...])
     depth = depth_of(gap, live[...])
-    ones = jnp.where(iota((SLOTS, 256), 0) < live[...], 1.0, 0.0)
-    got = scatter([depth * geom[c] for c in range(3)] + [ones], hots, xs, ys)
-    inverse = 1.0 / (1.0 + pick(sel[0:SLOTS], got[3]))
-    inverse_out[...] = inverse
-    normal = [got[c] * inverse for c in range(3)]
+    got = scatter([depth * geom[c] for c in range(3)], hots, xs, ys)
+    normal = [got[c] * inverse[...] for c in range(3)]
     for c in range(3):
         normal_out[c] = normal[c]
         moved_out[c] = jnp.zeros((SLOTS, 256), F32)
@@ -338,7 +369,7 @@
 
 
 def forward_kernel(got, edge, out):
-    sums = jnp.sum(got[:, OUTER:24, 0:128], axis=0)
+    sums = jnp.sum(got[:, 32:40, :], axis=0)
     lane = iota((8, 128), 1)
     sums = jnp.where((iota((8, 128), 0) == 0) & (lane > 17) & (lane < 20), sums, edge[...])
     for j in range(8):
@@ -353,7 +384,8 @@
     me = x * 4 + y
     outer = jnp.zeros((OUTER, 256), F32)
     for to, there in ((me - 4, x > 0), (me + 4, x < 3), (me - 1, y > 0), (me + 1, y < 3)):
-        reply = got[jnp.where(there, to, me), 0:OUTER, :]
+        at = jnp.where(there, to, me)
+        reply = jnp.concatenate([got[at, 0:OUTER, :], got[at, OUTER:32, :]], axis=1)
         outer = outer + jnp.where(there, reply, 0.0)
     lane = iota((SLOTS, 128), 1)
     above = unpack_edges(gotz[jnp.minimum(k + 1, 7)])
@@ -417,24 +449,24 @@
     return lax.axis_index("gx"), lax.axis_index("gy"), lax.axis_index(GZ)
 
 
+within = pltpu.with_memory_space_constraint
+
+
 def call(kernel, outs, args, scratch=(), inputs=False):
     vmem = pl.BlockSpec(memory_space=pltpu.VMEM)
+    hbm = pl.BlockSpec(memory_space=pltpu.HBM)
     return pl.pallas_call(
         kernel,
         out_shape=outs,
-        in_specs=[vmem] * len(args),
+        in_specs=[hbm if inputs else vmem] * len(args),
         out_specs=[vmem] * len(outs) if isinstance(outs, list) else vmem,
         scratch_shapes=list(scratch),
         compiler_params=pltpu.CompilerParams(vmem_limit_bytes=12 * 2**20),
-    )(*(args if inputs else [in_vmem(x) for x in args]))
+    )(*(args if inputs else [within(x, pltpu.VMEM) for x in args]))
 
 
 def shape(*dims, dtype=F32):
     return pltpu.VMEM(dims, dtype)
-
-
-def in_vmem(x):
-    return pltpu.with_memory_space_constraint(x, pltpu.VMEM)
 
 
 def shift(x, axis, up):
@@ -453,7 +485,7 @@
     live = live_blocks.reshape(1, 1)
     work = [pltpu.VMEM((2, 256, 128), F32)] * 2
 
-    face, ends = shape(224, 256), shape(264, 128)
+    face, ends = shape(224, 256), shape(40, 128)
     flat = shape(SLOTS, 256)
     flat_i = shape(SLOTS, 256, dtype=I32)
     few = shape(1, SLOTS, dtype=I32)
@@ -463,7 +495,8 @@
         + [ends] * 2
         + [shape(4, SLOTS, 256), shape(3, 256, 256), flat_i, flat_i, few, few]
         + [shape(1, 1, dtype=I32)],
-        [pos, node, far, geom, pline, fline, live],
+        [within(x, pltpu.HBM) for x in (pos, node, far, geom, pline, fline)] + [live],
+        [pltpu.VMEM((SLOTS, 4, 256), F32), pltpu.SemaphoreType.DMA((7,))],
         inputs=True,
     )
     xdn, xup, ydn, yup, zdn, zup, geom, pos, node, far, pline, fline, live = packed
@@ -476,8 +509,21 @@
     zlo = shift(zup, GZ, True)
     zhi = shift(zdn, GZ, False)
     triple = shape(3, SLOTS, 256)
-    outbound, edges = shape(16, 24, 256), shape(8, 128)
-    out, edge, change, gap, normal, moved, sel, selz, inverse, hots, first = call(
+    outbound, edges = shape(16, 40, 128), shape(8, 128)
+    gap, own, face, inverse, hots, first = call(
+        base_kernel,
+        [
+            flat,
+            shape(2 * SLOTS, 128),
+            shape(OUTER, 192, dtype=BF16),
+            flat,
+            shape(SLOTS, 256, 256, dtype=BF16),
+            flat,
+        ],
+        [pos, node, far, geom, pline, fline, live],
+        work,
+    )
+    out, edge, change, gap, normal, moved, sel, selz = call(
         first_kernel,
         [
             outbound,
@@ -488,11 +534,10 @@
             triple,
             shape(128, SLOTS, dtype=BF16),
             shape(OUTER, 2 * SLOTS, dtype=BF16),
-            flat,
-            shape(SLOTS, 256, 256, dtype=BF16),
-            flat,
         ],
-        [pos, node, far, geom, pline, fline, live, *requests, zlo, zhi],
+        [gap, own, face, inverse, far, geom, pline, live, node, hots, first]
+        + requests
+        + [zlo, zhi],
         work,
     )
     totals = []

time: 147 us -> 142 us (0.966)
  local copies, waits for them, and re-layouts: 4.85 us -> 0 us
  waiting for transfers between devices: 5.8 us -> 2.22 us
  Pallas kernels: 15.9 us -> 19.3 us
    unnamed x12 -> x0, local copies, waits for them, and re-layouts: 4.85 us -> none
    ppermute x6, waiting for transfers between devices: 5.8 us -> 2.22 us  [shift(): return lax.ppermute(x, axis, pairs if up else [(b, a) for a, b in pairs])]
    pallas_call x11 -> x12, Pallas kernels: 15.9 us -> 19.3 us  [call(): pl.pallas_call(kernel, out_shape=outs, in_specs=[hbm if inputs else vmem]...]
    all_to_all x4, blocking collectives: 53 us -> 50.5 us  [local(): got = lax.all_to_all(out, XY, 0, 0, tiled=True)]
  transfers between devices with their start and end apart: 6 -> 6, of which waited for: 2 -> 2; matrix products, arithmetic and copies ran while one was open for 0% -> 0% of each run, Pallas kernels for 0% -> 2%
where the time goes in v4:
time: 142 us; the launch traced here: 141 us
  blocking collectives  102 us (72%)
  Pallas kernels  19.3 us (14%)
  starting transfers between devices  16.3 us (11%)
  waiting for transfers between devices  2.22 us (2%)
    all_to_all x4, blocking collectives, local(): got = lax.all_to_all(out, XY, 0, 0, tiled=True)  50.5 us
    all_to_all x4, blocking collectives, local(): gotz = lax.all_to_all(out, GZ, 0, 0, tiled=True)  37.9 us
    pallas_call x12, Pallas kernels, call(): pl.pallas_call(kernel, out_shape=outs, in_specs=[hbm if inputs else vmem]...  19.3 us
    ppermute x6, starting transfers between devices, shift(): return lax.ppermute(x, axis, pairs if up else [(b, a) for a, b in pairs])  16.3 us
    all_to_all x1, blocking collectives, local(): got = lax.all_to_all(out, ALL, 0, 0, tiled=True)  13.3 us
  transfers between devices with their start and end apart: 6, of which 2 were waited for; matrix products, arithmetic and copies ran while one was open for 0% of the time, Pallas kernels for 2%

profile of v4, /device:TPU:1, one launch (start us, length us, event | category | flops | bytes accessed | tf_op | source)
XLA Modules:
  0.0 141.0 jit_solution(14794949393913086530)
XLA Ops:
  1.3 2.2 %shard_map.86 = (f32[224,256]{1,0:T(8,128)S(1)}, f32[224,256]{1,0:T(8,128)S(1)}, f32[224,256]{1,0:T(8,128)S(1)}, f32[224,256]{1,0:T(8,128)S(1)}, f32[40,128]{1,0...) custom-call(f32[3,256,256]{2,1,0:T(8,128)} %bitcast.15, ...), custom_call_target="tpu_custom_call" | custom-call | tf_op jit(solution)/shard_map/pallas_call | solution.py:458
  3.5 4.4 %collective-permute-start = (f32[224,256]{1,0:T(8,128)S(1)}, f32[224,256]{1,0:T(8,128)S(1)}, u32[]{:S(2)}, u32[]{:S(2)}) collective-permute-start(f32[224,256]{1,0:T(8,128)S(1)} %get-tuple-element.69), channel_id=1, source_target_pairs={{0,32},{32,64},{64,96},{1,33},{33,65},{65,97},{2,34},{34,66},{66,9... | collective-permute-start | bytes 688136 | tf_op jit(solution)/shard_map/ppermute | solution.py:475
  7.9 1.3 collective-permute-start.1
  9.2 3.2 %collective-permute-start.2 = (f32[224,256]{1,0:T(8,128)S(1)}, f32[224,256]{1,0:T(8,128)S(1)}, u32[]{:S(2)}, u32[]{:S(2)}) collective-permute-start(f32[224,256]{1,0:T(8,128)S(1)} %get-tuple-element.71), channel_id=1, source_target_pairs={{0,8},{8,16},{16,24},{1,9},{9,17},{17,25},{2,10},{10,18},{18,26},{... | collective-permute-start | bytes 688136 | tf_op jit(solution)/shard_map/ppermute | solution.py:475
  12.4 1.3 collective-permute-start.3
  13.7 4.2 %collective-permute-start.4 = (f32[40,128]{1,0:T(8,128)S(1)}, f32[40,128]{1,0:T(8,128)S(1)}, u32[]{:S(2)}, u32[]{:S(2)}) collective-permute-start(f32[40,128]{1,0:T(8,128)S(1)} %get-tuple-element.73), channel_id=1, source_target_pairs={{0,1},{1,2},{2,3},{3,4},{4,5},{5,6},{6,7},{8,9},{9,10},{10,11},{11... | collective-permute-start | bytes 61448 | tf_op jit(solution)/shard_map/ppermute | solution.py:475
  17.9 0.9 collective-permute-done.4.zlo
  18.8 1.9 %collective-permute-start.5 = (f32[40,128]{1,0:T(8,128)S(1)}, f32[40,128]{1,0:T(8,128)S(1)}, u32[]{:S(2)}, u32[]{:S(2)}) collective-permute-start(f32[40,128]{1,0:T(8,128)S(1)} %get-tuple-element.74), channel_id=1, source_target_pairs={{1,0},{2,1},{3,2},{4,3},{5,4},{6,5},{7,6},{9,8},{10,9},{11,10},{12... | collective-permute-start | bytes 61448 | tf_op jit(solution)/shard_map/ppermute | solution.py:475
  20.7 2.4 %shard_map.87 = (f32[32,256]{1,0:T(8,128)S(1)}, f32[64,128]{1,0:T(8,128)S(1)}, bf16[16,192]{1,0:T(8,128)(2,1)S(1)}, f32[32,256]{1,0:T(8,128)S(1)}, bf16[32,256,2...) custom-call(f32[3,256,256]{2,1,0:T(8,128)S(1)} %get-tuple-element.56.pos, s32[32,256]{1,0:T(8,128)S(1)} %get-tuple-element.57.node, ...), custom_call_target="tpu_custom_call" | custom-call | tf_op jit(solution)/shard_map/pallas_call | solution.py:458
  23.2 1.3 collective-permute-done.5.zhi
  24.5 0.0 collective-permute-done.xlo.rest_0_
  24.5 0.0 collective-permute-done.1.xhi.rest_1_
  24.5 0.0 collective-permute-done.2.ylo.rest_2_
  24.5 0.0 collective-permute-done.3.yhi.rest_3_
  24.5 2.9 %shard_map.88 = (f32[16,40,128]{2,1,0:T(8,128)S(1)}, f32[8,128]{1,0:T(8,128)S(1)}, f32[32,256]{1,0:T(8,128)S(1)}, f32[32,256]{1,0:T(8,128)S(1)}, f32[3,32,256]{2...) custom-call(f32[32,256]{1,0:T(8,128)S(1)} %get-tuple-element.63.gap_in, ...), custom_call_target="tpu_custom_call" | custom-call | tf_op jit(solution)/shard_map/pallas_call | solution.py:458
  27.4 17.2 %all_to_all.51.got = f32[16,40,128]{2,1,0:T(8,128)S(1)} all-to-all(f32[16,40,128]{2,1,0:T(8,128)S(1)} %get-tuple-element.81), channel_id=1, replica_groups=mesh['gx'=4,'gy'=4,'gz_0'=4,'gz_1'=2] {'gx','gy'}, dimensions={0} | all-to-all | bytes 655360 | tf_op jit(solution)/shard_map/all_to_all | solution.py:545
  44.7 11.1 %all_to_all.52.gotz = f32[8,8,128]{2,1,0:T(8,128)S(1)} all-to-all(f32[8,8,128]{2,1,0:T(8,128)S(1)} %shard_map.89), channel_id=1, replica_groups=mesh['gx'=4,'gy'=4,'gz_0'=4,'gz_1'=2] {'gz_0','gz_1'}, dimensions={0} | all-to-all | bytes 65536 | tf_op jit(solution)/shard_map/all_to_all | solution.py:547
  55.8 2.7 %shard_map.90 = (f32[16,40,128]{2,1,0:T(8,128)S(1)}, f32[8,128]{1,0:T(8,128)S(1)}, f32[32,256]{1,0:T(8,128)S(1)}, f32[32,256]{1,0:T(8,128)S(1)}, f32[8,128]{1,0:...) custom-call(f32[32,256]{1,0:T(8,128)S(1)} %get-tuple-element.75.gap, ...), custom_call_target="tpu_custom_call" | custom-call | tf_op jit(solution)/shard_map/pallas_call | solution.py:458
  58.5 11.1 %all_to_all.53.got = f32[16,40,128]{2,1,0:T(8,128)S(1)} all-to-all(f32[16,40,128]{2,1,0:T(8,128)S(1)} %get-tuple-element.87), channel_id=1, replica_groups=mesh['gx'=4,'gy'=4,'gz_0'=4,'gz_1'=2] {'gx','gy'}, dimensions={0} | all-to-all | bytes 655360 | tf_op jit(solution)/shard_map/all_to_all | solution.py:545
  69.7 8.9 %all_to_all.54.gotz = f32[8,8,128]{2,1,0:T(8,128)S(1)} all-to-all(f32[8,8,128]{2,1,0:T(8,128)S(1)} %shard_map.91), channel_id=1, replica_groups=mesh['gx'=4,'gy'=4,'gz_0'=4,'gz_1'=2] {'gz_0','gz_1'}, dimensions={0} | all-to-all | bytes 65536 | tf_op jit(solution)/shard_map/all_to_all | solution.py:547
  78.6 2.7 %shard_map.92 = (f32[16,40,128]{2,1,0:T(8,128)S(1)}, f32[8,128]{1,0:T(8,128)S(1)}, f32[32,256]{1,0:T(8,128)S(1)}, f32[32,256]{1,0:T(8,128)S(1)}, f32[8,128]{1,0:...) custom-call(f32[32,256]{1,0:T(8,128)S(1)} %get-tuple-element.83.gap, ...), custom_call_target="tpu_custom_call" | custom-call | tf_op jit(solution)/shard_map/pallas_call | solution.py:458
  81.3 11.1 %all_to_all.55.got = f32[16,40,128]{2,1,0:T(8,128)S(1)} all-to-all(f32[16,40,128]{2,1,0:T(8,128)S(1)} %get-tuple-element.93), channel_id=1, replica_groups=mesh['gx'=4,'gy'=4,'gz_0'=4,'gz_1'=2] {'gx','gy'}, dimensions={0} | all-to-all | bytes 655360 | tf_op jit(solution)/shard_map/all_to_all | solution.py:545
  92.4 8.9 %all_to_all.56.gotz = f32[8,8,128]{2,1,0:T(8,128)S(1)} all-to-all(f32[8,8,128]{2,1,0:T(8,128)S(1)} %shard_map.93), channel_id=1, replica_groups=mesh['gx'=4,'gy'=4,'gz_0'=4,'gz_1'=2] {'gz_0','gz_1'}, dimensions={0} | all-to-all | bytes 65536 | tf_op jit(solution)/shard_map/all_to_all | solution.py:547
  101.3 2.7 %shard_map.94 = (f32[16,40,128]{2,1,0:T(8,128)S(1)}, f32[8,128]{1,0:T(8,128)S(1)}, f32[32,256]{1,0:T(8,128)S(1)}, f32[32,256]{1,0:T(8,128)S(1)}, f32[8,128]{1,0:...) custom-call(f32[32,256]{1,0:T(8,128)S(1)} %get-tuple-element.89.gap, ...), custom_call_target="tpu_custom_call" | custom-call | tf_op jit(solution)/shard_map/pallas_call | solution.py:458
  104.0 11.1 %all_to_all.57.got = f32[16,40,128]{2,1,0:T(8,128)S(1)} all-to-all(f32[16,40,128]{2,1,0:T(8,128)S(1)} %get-tuple-element.99), channel_id=1, replica_groups=mesh['gx'=4,'gy'=4,'gz_0'=4,'gz_1'=2] {'gx','gy'}, dimensions={0} | all-to-all | bytes 655360 | tf_op jit(solution)/shard_map/all_to_all | solution.py:545
  115.2 8.9 %all_to_all.58.gotz = f32[8,8,128]{2,1,0:T(8,128)S(1)} all-to-all(f32[8,8,128]{2,1,0:T(8,128)S(1)} %shard_map.95), channel_id=1, replica_groups=mesh['gx'=4,'gy'=4,'gz_0'=4,'gz_1'=2] {'gz_0','gz_1'}, dimensions={0} | all-to-all | bytes 65536 | tf_op jit(solution)/shard_map/all_to_all | solution.py:547
  124.1 2.2 %shard_map.96 = (f32[128,128]{1,0:T(8,128)S(1)}, f32[8,128]{1,0:T(8,128)S(1)}, f32[3,32,256]{2,1,0:T(8,128)S(1)}, f32[3,32,256]{2,1,0:T(8,128)S(1)}) custom-call(f32[32,256]{1,0:T(8,128)S(1)} %get-tuple-element.95.gap, f32[32,256]{1,0:T(8,128)S(1)} %get-tuple-element.96.change, f32[3,32,256]{2,1,0:T(8,128)S(1)} %get-tuple-element.97.normal, ...), custom_call_target="tpu_custom_call" | custom-call | tf_op jit(solution)/shard_map/pallas_call | solution.py:458
  126.3 13.3 %all_to_all.59 = f32[128,1,128]{2,1,0:T(1,128)S(1)} all-to-all(f32[128,1,128]{2,1,0:T(1,128)S(1)} %bitcast.14), channel_id=1, replica_groups=mesh['gx'=4,'gy'=4,'gz_0'=4,'gz_1'=2] {'gx','gy','gz_0','gz_1'}, dimensions={0} | all-to-all | bytes 131072 | tf_op jit(solution)/shard_map/all_to_all | solution.py:569
  139.6 1.3 shard_map.97
  (4 shorter events, 0.1 us)
Async XLA Ops:
  3.5 21.0 %collective-permute-start = (f32[224,256]{1,0:T(8,128)S(1)}, f32[224,256]{1,0:T(8,128)S(1)}, u32[]{:S(2)}, u32[]{:S(2)}) collective-permute-start(f32[224,256]{1,0:T(8,128)S(1)} %get-tuple-element.69), channel_id=1, source_target_pairs={{0,32},{32,64},{64,96},{1,33},{33,65},{65,97},{2,34},{34,66},{66,9... | collective-permute-start | bytes 688136 | tf_op jit(solution)/shard_map/ppermute | solution.py:475
  7.9 16.6 %collective-permute-start.1 = (f32[224,256]{1,0:T(8,128)S(1)}, f32[224,256]{1,0:T(8,128)S(1)}, u32[]{:S(2)}, u32[]{:S(2)}) collective-permute-start(f32[224,256]{1,0:T(8,128)S(1)} %get-tuple-element.70), channel_id=1, source_target_pairs={{32,0},{64,32},{96,64},{33,1},{65,33},{97,65},{34,2},{66,34},{98,6... | collective-permute-start | bytes 688136 | tf_op jit(solution)/shard_map/ppermute | solution.py:475
  9.2 15.3 %collective-permute-start.2 = (f32[224,256]{1,0:T(8,128)S(1)}, f32[224,256]{1,0:T(8,128)S(1)}, u32[]{:S(2)}, u32[]{:S(2)}) collective-permute-start(f32[224,256]{1,0:T(8,128)S(1)} %get-tuple-element.71), channel_id=1, source_target_pairs={{0,8},{8,16},{16,24},{1,9},{9,17},{17,25},{2,10},{10,18},{18,26},{... | collective-permute-start | bytes 688136 | tf_op jit(solution)/shard_map/ppermute | solution.py:475
  12.4 12.1 %collective-permute-start.3 = (f32[224,256]{1,0:T(8,128)S(1)}, f32[224,256]{1,0:T(8,128)S(1)}, u32[]{:S(2)}, u32[]{:S(2)}) collective-permute-start(f32[224,256]{1,0:T(8,128)S(1)} %get-tuple-element.72), channel_id=1, source_target_pairs={{8,0},{16,8},{24,16},{9,1},{17,9},{25,17},{10,2},{18,10},{26,18},{... | collective-permute-start | bytes 688136 | tf_op jit(solution)/shard_map/ppermute | solution.py:475
  13.7 5.1 %collective-permute-start.4 = (f32[40,128]{1,0:T(8,128)S(1)}, f32[40,128]{1,0:T(8,128)S(1)}, u32[]{:S(2)}, u32[]{:S(2)}) collective-permute-start(f32[40,128]{1,0:T(8,128)S(1)} %get-tuple-element.73), channel_id=1, source_target_pairs={{0,1},{1,2},{2,3},{3,4},{4,5},{5,6},{6,7},{8,9},{9,10},{10,11},{11... | collective-permute-start | bytes 61448 | tf_op jit(solution)/shard_map/ppermute | solution.py:475
  18.8 5.7 %collective-permute-start.5 = (f32[40,128]{1,0:T(8,128)S(1)}, f32[40,128]{1,0:T(8,128)S(1)}, u32[]{:S(2)}, u32[]{:S(2)}) collective-permute-start(f32[40,128]{1,0:T(8,128)S(1)} %get-tuple-element.74), channel_id=1, source_target_pairs={{1,0},{2,1},{3,2},{4,3},{5,4},{6,5},{7,6},{9,8},{10,9},{11,10},{12... | collective-permute-start | bytes 61448 | tf_op jit(solution)/shard_map/ppermute | solution.py:475
